TPU v7x, 32 devices: a whole 2x2x4 slice. The times are simulated.
32 devices in a mesh: seq: 8 (over y, x, core), ad: 4 (over z).
Axes of the slice: x: 2, y: 2, z: 4, core: 2. Of those that a mesh axis runs over, the one named last changes fastest.
Arguments:
- tokens: bfloat16 [4, 2048, 2048], P('ad', 'seq'), may hold values from -6 to 6
- out_grad: bfloat16 [4, 2048, 2048], P('ad', 'seq'), may hold values from -6 to 6
- block_role: int32 [4, 16], P('ad'), may hold values from 0 to 15, each once within a row
- adapter_of: int32 [4, 8], P('ad'), may hold values from 0 to 7
- attn_gain: float32 [2048], replicated, may hold values from 0.1 to 1.9
- ffn_gain: float32 [2048], replicated, may hold values from 0.1 to 1.9
- wqkv: bfloat16 [2048, 4096], P(('seq', 'ad')), may hold values from -0.125 to 0.125
- wo: bfloat16 [2048, 2048], P(('seq', 'ad')), may hold values from -0.5 to 0.5
- ffn: bfloat16 [2048, 3, 8192], P(('seq', 'ad')), may hold values from -0.125 to 0.125
- qkv_a: bfloat16 [8, 16, 2048], P('ad'), may hold values from -0.125 to 0.125
- qkv_b: bfloat16 [8, 16, 4096], P('ad'), may hold values from -1.5 to 1.5
- out_a: bfloat16 [8, 16, 2048], P('ad'), may hold values from -0.5 to 0.5
- out_b: bfloat16 [8, 16, 2048], P('ad'), may hold values from -1.5 to 1.5
- ffn_in_a: bfloat16 [8, 2, 16, 2048], P('ad'), may hold values from -0.125 to 0.125
- ffn_in_b: bfloat16 [8, 2, 16, 8192], P('ad'), may hold values from -1.5 to 1.5
- ffn_out_a: bfloat16 [8, 16, 8192], P('ad'), may hold values from -0.0625 to 0.0625
- ffn_out_b: bfloat16 [8, 16, 2048], P('ad'), may hold values from -1.5 to 1.5
Outputs:
- output: bfloat16 [4, 2048, 2048], P('ad', 'seq')
- input_grad: float32 [4, 2048, 2048], P('ad', 'seq')
- qkv_a_grad: float32 [8, 16, 2048], P('ad')
- qkv_b_grad: float32 [8, 16, 4096], P('ad')
- out_a_grad: float32 [8, 16, 2048], P('ad')
- out_b_grad: float32 [8, 16, 2048], P('ad')
- ffn_in_a_grad: float32 [8, 2, 16, 2048], P('ad')
- ffn_in_b_grad: float32 [8, 2, 16, 8192], P('ad')
- ffn_out_a_grad: float32 [8, 16, 8192], P('ad')
- ffn_out_b_grad: float32 [8, 16, 2048], P('ad')
Inputs may be any that keep to these rules, and one draw needn't show every extreme that they name: `block_role`: each group's row names every role once; roles below 8 are the prompt's blocks in order, the others continuations.
All inputs are finite; a program needn't handle non-finite values.
Results may differ from a plain program's by a relative error of at most 0.025.
Values may be sent and summed in bfloat16 or wider, within the bound.
A program may use at most 256 MiB of HBM per device.

v0:
```python
import math

import jax
import jax.numpy as jnp
from jax import lax
from jax.sharding import PartitionSpec as P

QUERY_HEADS = 16
KEY_VALUE_HEADS = 8
HEAD_SIZE = 128
FF = 8192
R = 16
NA = 8
PBLK = 8
CONTS = 8
BLOCK = 128
SLOTS = 16


eps_norm = 1e-05
rope_base = 1000000.0


def product(matrix_a, matrix_b):
    return jnp.dot(matrix_a, matrix_b, preferred_element_type=jnp.float32)


def product_nt(matrix_a, matrix_b):
    return lax.dot_general(
        matrix_a, matrix_b, (((1,), (1,)), ((), ())), preferred_element_type=jnp.float32
    )


def product_tn(matrix_a, matrix_b):
    return lax.dot_general(
        matrix_a, matrix_b, (((0,), (0,)), ((), ())), preferred_element_type=jnp.float32
    )


def stacked(matrix_a):
    return matrix_a.reshape(matrix_a.shape[0] * matrix_a.shape[1], matrix_a.shape[2])


def norm_forward(values, gain):
    inverse = lax.rsqrt(jnp.mean(values * values, axis=-1, keepdims=True) + eps_norm)
    return (values * inverse * gain, inverse)


def norm_backward(values, inverse, gain, grads):
    weighted = grads * gain
    return inverse * weighted - values * (inverse * inverse * inverse) * jnp.mean(
        values * weighted, axis=-1, keepdims=True
    )


def rope_tables(token_position, size_head):
    half_size = size_head // 2
    frequency = jnp.exp(
        jnp.arange(half_size, dtype=jnp.float32) * (-2.0 * math.log(rope_base) / size_head)
    )
    angles = token_position.astype(jnp.float32)[:, None] * frequency[None, :]
    return (jnp.cos(angles)[:, None, :], jnp.sin(angles)[:, None, :])


def rotate(values, cosine, sine_table):
    half_size = values.shape[-1] // 2
    leading = values[..., :half_size]
    trailing = values[..., half_size:]
    return jnp.concatenate(
        [leading * cosine - trailing * sine_table, trailing * cosine + leading * sine_table],
        axis=-1,
    )


def rotate_back(grads, cosine, sine_table):
    half_size = grads.shape[-1] // 2
    leading = grads[..., :half_size]
    trailing = grads[..., half_size:]
    return jnp.concatenate(
        [leading * cosine + trailing * sine_table, trailing * cosine - leading * sine_table],
        axis=-1,
    )


def token_layout(role_row, owner_row):
    role_tok = jnp.repeat(role_row, BLOCK)
    offset = jnp.arange(SLOTS * BLOCK, dtype=jnp.int32) % BLOCK
    is_later = role_tok >= PBLK
    token_position = jnp.where(is_later, PBLK * BLOCK + offset, role_tok * BLOCK + offset)
    matches = (role_tok - PBLK)[:, None] == jnp.arange(CONTS, dtype=jnp.int32)[None, :]
    owner_tok = jnp.max(jnp.where(matches, owner_row[None, :], -1), axis=1)
    column_owner = jnp.arange(NA * R, dtype=jnp.int32) // R
    select = (owner_tok[:, None] == column_owner[None, :]).astype(jnp.float32)
    return (role_tok, token_position, select)


def visible_mask(query_role, query_pos, key_role, key_pos):
    causal = key_pos[None, :] <= query_pos[:, None]
    prompt_key = (key_role[None, :] < PBLK) & ((query_role[:, None] >= PBLK) | causal)
    own_key = (key_role[None, :] >= PBLK) & (key_role[None, :] == query_role[:, None]) & causal
    return prompt_key | own_key


def local(
    tokens,
    out_grad,
    block_role,
    adapter_of,
    attn_gain,
    ffn_gain,
    wqkv,
    wo,
    ffn,
    qkv_a,
    qkv_b,
    out_a,
    out_b,
    ffn_in_a,
    ffn_in_b,
    ffn_out_a,
    ffn_out_b,
):
    rows_per_device = tokens.shape[1]
    width = tokens.shape[2]
    ranks = NA * R
    heads_per_group = QUERY_HEADS // KEY_VALUE_HEADS
    score_scale = 1.0 / math.sqrt(HEAD_SIZE)
    ff_part = FF // lax.axis_size("ad")
    ff_start = lax.axis_index("ad") * ff_part
    row_start = lax.axis_index("seq") * rows_per_device
    role_tok, token_position, select_all = token_layout(block_role[0], adapter_of[0])
    my_role = lax.dynamic_slice_in_dim(role_tok, row_start, rows_per_device)
    my_position = lax.dynamic_slice_in_dim(token_position, row_start, rows_per_device)
    select_f = lax.dynamic_slice_in_dim(select_all, row_start, rows_per_device, 0)
    select_b = select_f.astype(jnp.bfloat16)
    select_pair = jnp.concatenate([select_f, select_f], axis=1)
    visible = visible_mask(my_role, my_position, role_tok, token_position)
    cosine, sine_table = rope_tables(my_position, HEAD_SIZE)
    stacks = (
        lax.all_gather(qkv_a, "ad", axis=0, tiled=True),
        lax.all_gather(qkv_b, "ad", axis=0, tiled=True),
        lax.all_gather(out_a, "ad", axis=0, tiled=True),
        lax.all_gather(out_b, "ad", axis=0, tiled=True),
        lax.all_gather(ffn_in_a, "ad", axis=0, tiled=True),
        lax.all_gather(ffn_in_b, "ad", axis=0, tiled=True),
        lax.all_gather(ffn_out_a, "ad", axis=0, tiled=True),
        lax.all_gather(ffn_out_b, "ad", axis=0, tiled=True),
    )
    qkv_enter = stacked(stacks[0])
    qkv_leave = stacked(stacks[1])
    out_enter = stacked(stacks[2])
    out_leave = stacked(stacks[3])
    gate_enter = stacked(stacks[4][:, 0])
    upper_enter = stacked(stacks[4][:, 1])
    leave_part = lax.dynamic_slice_in_dim(stacks[5], ff_start, ff_part, 3)
    gate_leave = stacked(leave_part[:, 0])
    upper_leave = stacked(leave_part[:, 1])
    down_enter = stacked(lax.dynamic_slice_in_dim(stacks[6], ff_start, ff_part, 2))
    down_leave = stacked(stacks[7])
    inputs_f = tokens[0].astype(jnp.float32)
    normed, inverse_attn = norm_forward(inputs_f, attn_gain)
    normed_attn = normed.astype(jnp.bfloat16)
    rank_qkv = product_nt(normed_attn, qkv_enter).astype(jnp.bfloat16) * select_b
    projected_rows = product(rank_qkv, qkv_leave) + product(
        normed_attn, lax.all_gather(wqkv, ("seq", "ad"), axis=0, tiled=True)
    )
    projected_rows = projected_rows.reshape(
        rows_per_device, KEY_VALUE_HEADS, heads_per_group + 2, HEAD_SIZE
    )
    query_rows = rotate(
        projected_rows[:, :, :heads_per_group].reshape(rows_per_device, QUERY_HEADS, HEAD_SIZE),
        cosine,
        sine_table,
    ).astype(jnp.bfloat16)
    heads_of_query = query_rows.reshape(
        rows_per_device, KEY_VALUE_HEADS, heads_per_group, HEAD_SIZE
    ).transpose(1, 2, 0, 3)
    key_local = (
        rotate(projected_rows[:, :, heads_per_group], cosine, sine_table)
        .astype(jnp.bfloat16)
        .transpose(1, 0, 2)
    )
    value_local = projected_rows[:, :, heads_per_group + 1].astype(jnp.bfloat16).transpose(1, 0, 2)
    keys_group, values_group = (
        lax.all_gather(key_local, "seq", axis=1, tiled=True),
        lax.all_gather(value_local, "seq", axis=1, tiled=True),
    )

    def head_scores(query_head, key_head):
        scores = (
            jnp.einsum("jqd,kd->jqk", query_head, key_head, preferred_element_type=jnp.float32)
            * score_scale
        )
        return jnp.where(visible[None], scores, -1e30)

    def head_forward(head_inputs):
        query_head, key_head, value_head = head_inputs
        scores = head_scores(query_head, key_head)
        top_score = jnp.max(scores, axis=-1, keepdims=True)
        exponent = jnp.exp(scores - top_score)
        totals = jnp.sum(exponent, axis=-1, keepdims=True)
        probability = (exponent / totals).astype(jnp.bfloat16)
        result = jnp.einsum(
            "jqk,kd->jqd", probability, value_head, preferred_element_type=jnp.float32
        )
        return (result, (top_score + jnp.log(totals))[..., 0])

    heads_out, log_totals = lax.map(head_forward, (heads_of_query, keys_group, values_group))
    attn = (
        heads_out.transpose(2, 0, 1, 3)
        .reshape(rows_per_device, QUERY_HEADS * HEAD_SIZE)
        .astype(jnp.bfloat16)
    )
    rank_out = product_nt(attn, out_enter).astype(jnp.bfloat16) * select_b
    branch = product(rank_out, out_leave) + product(
        attn, lax.all_gather(wo, ("seq", "ad"), axis=0, tiled=True)
    )
    residual = inputs_f + branch
    normed_two, inverse_ffn = norm_forward(residual, ffn_gain)
    normed_ffn = normed_two.astype(jnp.bfloat16)
    rank_ffn = jnp.concatenate(
        [product_nt(normed_ffn, gate_enter), product_nt(normed_ffn, upper_enter)], axis=1
    ).astype(jnp.bfloat16) * jnp.concatenate([select_b, select_b], axis=1)

    def fetch_ffn():
        regrouped = lax.all_to_all(ffn, "ad", split_axis=2, concat_axis=0, tiled=True)
        return lax.all_gather(regrouped, "seq", axis=0, tiled=True)

    ffn_local = fetch_ffn()
    normed_all, rank_all = (
        lax.all_gather(normed_ffn, "ad", axis=0, tiled=True),
        lax.all_gather(rank_ffn, "ad", axis=0, tiled=True),
    )
    gate_val = product(normed_all, ffn_local[:, 0]) + product(rank_all[:, :ranks], gate_leave)
    upper_val = product(normed_all, ffn_local[:, 1]) + product(rank_all[:, ranks:], upper_leave)
    silu_gate = jax.nn.silu(gate_val)
    hidden = (silu_gate * upper_val).astype(jnp.bfloat16)
    down_summed = lax.psum_scatter(
        jnp.concatenate(
            [product_nt(hidden, ffn_local[:, 2]), product_nt(hidden, down_enter)], axis=1
        ).astype(jnp.bfloat16),
        "ad",
        scatter_dimension=0,
        tiled=True,
    ).astype(jnp.float32)
    rank_down = down_summed[:, width:].astype(jnp.bfloat16) * select_b
    result_f = residual + down_summed[:, :width] + product(rank_down, down_leave)
    output = result_f.astype(jnp.bfloat16)[None]
    grad_down = out_grad[0]
    grad_f = grad_down.astype(jnp.float32)
    down_leave_grad = product_tn(rank_down, grad_down)
    d_rank_down = (product_nt(grad_down, down_leave) * select_f).astype(jnp.bfloat16)
    ffn_back = fetch_ffn()
    grad_all, d_rank_down_all = (
        lax.all_gather(grad_down, "ad", axis=0, tiled=True),
        lax.all_gather(d_rank_down, "ad", axis=0, tiled=True),
    )
    d_hidden = product(grad_all, ffn_back[:, 2]) + product(d_rank_down_all, down_enter)
    down_enter_part = product_tn(d_rank_down_all, hidden)
    sigma = jax.nn.sigmoid(gate_val)
    d_gate = (d_hidden * upper_val * sigma * (1.0 + gate_val * (1.0 - sigma))).astype(jnp.bfloat16)
    d_upper = (d_hidden * silu_gate).astype(jnp.bfloat16)
    gate_leave_part = product_tn(rank_all[:, :ranks], d_gate)
    upper_leave_part = product_tn(rank_all[:, ranks:], d_upper)
    back_summed = lax.psum_scatter(
        jnp.concatenate(
            [
                product_nt(d_gate, ffn_back[:, 0]) + product_nt(d_upper, ffn_back[:, 1]),
                product_nt(d_gate, gate_leave),
                product_nt(d_upper, upper_leave),
            ],
            axis=1,
        ),
        "ad",
        scatter_dimension=0,
        tiled=True,
    )
    d_rank_ffn = (back_summed[:, width:] * select_pair).astype(jnp.bfloat16)
    d_normed_ffn = (
        back_summed[:, :width]
        + product(d_rank_ffn[:, :ranks], gate_enter)
        + product(d_rank_ffn[:, ranks:], upper_enter)
    )
    d_residual = grad_f + norm_backward(residual, inverse_ffn, ffn_gain, d_normed_ffn)
    d_branch = d_residual.astype(jnp.bfloat16)
    out_leave_grad = product_tn(rank_out, d_branch)
    d_rank_out = (product_nt(d_branch, out_leave) * select_f).astype(jnp.bfloat16)
    out_enter_grad = product_tn(d_rank_out, attn)
    attention_grad = (
        product_nt(d_branch, lax.all_gather(wo, ("seq", "ad"), axis=0, tiled=True))
        + product(d_rank_out, out_enter)
    ).astype(jnp.bfloat16)
    heads_grad = attention_grad.reshape(
        rows_per_device, KEY_VALUE_HEADS, heads_per_group, HEAD_SIZE
    ).transpose(1, 2, 0, 3)

    def head_backward(head_inputs):
        query_head, key_head, value_head, grad_head, log_head = head_inputs
        scores = head_scores(query_head, key_head)
        probability = jnp.exp(scores - log_head[..., None])
        grad_prob = jnp.einsum(
            "jqd,kd->jqk", grad_head, value_head, preferred_element_type=jnp.float32
        )
        centre = jnp.sum(probability * grad_prob, axis=-1, keepdims=True)
        grad_score = (probability * (grad_prob - centre) * score_scale).astype(jnp.bfloat16)
        grad_query = jnp.einsum(
            "jqk,kd->jqd", grad_score, key_head, preferred_element_type=jnp.float32
        )
        grad_key = jnp.einsum(
            "jqk,jqd->kd", grad_score, query_head, preferred_element_type=jnp.float32
        )
        grad_value = jnp.einsum(
            "jqk,jqd->kd",
            probability.astype(jnp.bfloat16),
            grad_head,
            preferred_element_type=jnp.float32,
        )
        key_own, value_own = (
            lax.psum_scatter(
                grad_key.astype(jnp.bfloat16), "seq", scatter_dimension=0, tiled=True
            ).astype(jnp.float32),
            lax.psum_scatter(
                grad_value.astype(jnp.bfloat16), "seq", scatter_dimension=0, tiled=True
            ).astype(jnp.float32),
        )
        return (grad_query, key_own, value_own)

    grad_queries, grad_keys, grad_values = lax.map(
        head_backward, (heads_of_query, keys_group, values_group, heads_grad, log_totals)
    )
    query_gradient = rotate_back(
        grad_queries.transpose(2, 0, 1, 3).reshape(rows_per_device, QUERY_HEADS, HEAD_SIZE),
        cosine,
        sine_table,
    )
    key_gradient = rotate_back(grad_keys.transpose(1, 0, 2), cosine, sine_table)
    value_gradient = grad_values.transpose(1, 0, 2)
    d_projected = (
        jnp.concatenate(
            [
                query_gradient.reshape(
                    rows_per_device, KEY_VALUE_HEADS, heads_per_group, HEAD_SIZE
                ),
                key_gradient[:, :, None],
                value_gradient[:, :, None],
            ],
            axis=2,
        )
        .reshape(rows_per_device, -1)
        .astype(jnp.bfloat16)
    )
    qkv_leave_grad = product_tn(rank_qkv, d_projected)
    d_rank_qkv = (product_nt(d_projected, qkv_leave) * select_f).astype(jnp.bfloat16)
    qkv_enter_grad = product_tn(d_rank_qkv, normed_attn)
    d_normed_attn = product_nt(
        d_projected, lax.all_gather(wqkv, ("seq", "ad"), axis=0, tiled=True)
    ) + product(d_rank_qkv, qkv_enter)
    input_grad = (d_residual + norm_backward(inputs_f, inverse_attn, attn_gain, d_normed_attn))[
        None
    ]
    in_enter_grad = jnp.stack(
        [
            product_tn(d_rank_ffn[:, :ranks], normed_ffn).reshape(NA, R, width),
            product_tn(d_rank_ffn[:, ranks:], normed_ffn).reshape(NA, R, width),
        ],
        axis=1,
    )
    in_leave_part = jnp.stack(
        [gate_leave_part.reshape(NA, R, ff_part), upper_leave_part.reshape(NA, R, ff_part)], axis=1
    )
    in_leave_grad = lax.dynamic_update_slice(
        jnp.zeros((NA, 2, R, FF), jnp.float32), in_leave_part, (0, 0, 0, ff_start)
    )
    down_enter_grad = lax.dynamic_update_slice(
        jnp.zeros((NA, R, FF), jnp.float32),
        down_enter_part.reshape(NA, R, ff_part),
        (0, 0, ff_start),
    )
    grad_terms = (
        qkv_enter_grad.reshape(NA, R, width),
        qkv_leave_grad.reshape(NA, R, -1),
        out_enter_grad.reshape(NA, R, -1),
        out_leave_grad.reshape(NA, R, width),
        in_enter_grad,
        in_leave_grad,
        down_enter_grad,
        down_leave_grad.reshape(NA, R, width),
    )
    shares = (
        lax.psum_scatter(
            grad_terms[0].astype(jnp.bfloat16), "ad", scatter_dimension=0, tiled=True
        ).astype(jnp.float32),
        lax.psum_scatter(
            grad_terms[1].astype(jnp.bfloat16), "ad", scatter_dimension=0, tiled=True
        ).astype(jnp.float32),
        lax.psum_scatter(
            grad_terms[2].astype(jnp.bfloat16), "ad", scatter_dimension=0, tiled=True
        ).astype(jnp.float32),
        lax.psum_scatter(
            grad_terms[3].astype(jnp.bfloat16), "ad", scatter_dimension=0, tiled=True
        ).astype(jnp.float32),
        lax.psum_scatter(
            grad_terms[4].astype(jnp.bfloat16), "ad", scatter_dimension=0, tiled=True
        ).astype(jnp.float32),
        lax.psum_scatter(
            grad_terms[5].astype(jnp.bfloat16), "ad", scatter_dimension=0, tiled=True
        ).astype(jnp.float32),
        lax.psum_scatter(
            grad_terms[6].astype(jnp.bfloat16), "ad", scatter_dimension=0, tiled=True
        ).astype(jnp.float32),
        lax.psum_scatter(
            grad_terms[7].astype(jnp.bfloat16), "ad", scatter_dimension=0, tiled=True
        ).astype(jnp.float32),
    )
    mine = list(
        (
            lax.psum(shares[0].astype(jnp.bfloat16), "seq").astype(jnp.float32),
            lax.psum(shares[1].astype(jnp.bfloat16), "seq").astype(jnp.float32),
            lax.psum(shares[2].astype(jnp.bfloat16), "seq").astype(jnp.float32),
            lax.psum(shares[3].astype(jnp.bfloat16), "seq").astype(jnp.float32),
            lax.psum(shares[4].astype(jnp.bfloat16), "seq").astype(jnp.float32),
            lax.psum(shares[5].astype(jnp.bfloat16), "seq").astype(jnp.float32),
            lax.psum(shares[6].astype(jnp.bfloat16), "seq").astype(jnp.float32),
            lax.psum(shares[7].astype(jnp.bfloat16), "seq").astype(jnp.float32),
        )
    )
    return (
        output,
        input_grad,
        mine[0],
        mine[1],
        mine[2],
        mine[3],
        mine[4],
        mine[5],
        mine[6],
        mine[7],
    )


def solution(mesh):
    return jax.shard_map(
        local,
        mesh=mesh,
        in_specs=(
            P("ad", "seq", None),
            P("ad", "seq", None),
            P("ad", None),
            P("ad", None),
            P(),
            P(),
            P(("seq", "ad"), None),
            P(("seq", "ad"), None),
            P(("seq", "ad"), None, None),
            P("ad", None, None),
            P("ad", None, None),
            P("ad", None, None),
            P("ad", None, None),
            P("ad", None, None, None),
            P("ad", None, None, None),
            P("ad", None, None),
            P("ad", None, None),
        ),
        out_specs=(
            P("ad", "seq", None),
            P("ad", "seq", None),
            P("ad", None, None),
            P("ad", None, None),
            P("ad", None, None),
            P("ad", None, None),
            P("ad", None, None, None),
            P("ad", None, None, None),
            P("ad", None, None),
            P("ad", None, None),
        ),
        check_vma=False,
    )
```

profile of v0, /device:TPU:0, one launch (start us, length us, event | category | flops | bytes accessed | tf_op | source)
XLA Modules:
  0.0 2265.6 jit_solution(10975375284473292963)
XLA Ops:
  34.3 96.2 %all-gather.15.cloned.1.call-done = bf16[2048,4096]{1,0:T(8,128)(2,1)} async-done(((bf16[64,4096]{1,0:T(8,128)(2,1)}), bf16[2048,4096]{1,0:T(8,128)(2,1)}) %all-gather.15.cloned.1.call-update) | async-done | bytes 16777232 | tf_op jit(solution)/shard_map/all_gather | solution.py:165
  218.1 31.7 %all-gather.19.cloned.1.call-done = bf16[8,2048,128]{2,1,0:T(8,128)(2,1)} async-done(((bf16[8,256,128]{2,1,0:T(8,128)(2,1)}), bf16[8,2048,128]{2,1,0:T(8,128)(2,1)}) %all-gather.19.cloned.1.call-update) | async-done | bytes 4194320 | tf_op jit(solution)/shard_map/all_gather | solution.py:186
  249.7 59.3 %while.28 = (s32[]{:T(128)}, bf16[8,2,256,128]{2,3,1,0:T(8,128)(2,1)S(1)}, f32[8,2,256]{2,1,0:T(2,128)}, bf16[8,2,256,128]{3,2,1,0:T(8,128)(2,1)}, bf16[8,2048,1...) while((s32[]{:T(128)}, ...), condition=%wide.region_5.6_spmd.clone, body=%wide.region_2.5_spmd.clone.sunk | while | flops 553123328 | bytes 16163717 | solution.py:208
  355.8 116.0 %all_to_all.23 = bf16[4,2,196608]{2,1,0:T(2,128)(2,1)} all-to-all(bf16[4,2,196608]{2,1,0:T(2,128)(2,1)S(1)} %reshape.324), channel_id=1, replica_groups=mesh['seq'=8,'ad'=4] {'ad'}, dimensions={0} | all-to-all | bytes 6291456 | tf_op jit(solution)/shard_map/all_to_all | solution.py:226
  575.2 55.7 %all-gather.23.cloned.1.call-done = bf16[1024,2048]{0,1:T(8,128)(2,1)} async-done(((bf16[256,2048]{0,1:T(8,128)(2,1)}), bf16[1024,2048]{0,1:T(8,128)(2,1)}) %all-gather.23.cloned.1.call-update) | async-done | bytes 4194320 | tf_op jit(solution)/shard_map/all_gather | solution.py:231
  630.9 124.3 %all-gather.25.cloned.1.call-done = bf16[2048,3,2048]{2,0,1:T(8,128)(2,1)} async-done(((bf16[256,3,2048]{2,0,1:T(8,128)(2,1)}), bf16[2048,3,2048]{2,0,1:T(8,128)(2,1)}) %all-gather.25.cloned.1.call-update) | async-done | bytes 25165840 | tf_op jit(solution)/shard_map/all_gather | solution.py:227
  771.1 66.5 %all-gather.33.cloned.1.call-done = bf16[1,1024,2048]{2,1,0:T(8,128)(2,1)} async-done(((bf16[1,256,2048]{2,1,0:T(8,128)(2,1)}), bf16[1,1024,2048]{2,1,0:T(8,128)(2,1)}) %all-gather.33.cloned.1.call-update) | async-done | bytes 4194320 | tf_op jit(solution)/shard_map/all_gather | solution.py:255
  853.3 24.3 %multiply_convert_fusion.2 = (bf16[1024,2048]{1,0:T(8,128)(2,1)}, bf16[1024,2048]{1,0:T(8,128)(2,1)}, bf16[1024,2048]{1,0:T(8,128)(2,1)}) fusion(f32[1024,2048]{1,0:T(8,128)} %fusion.79, f32[1024,2048]{1,0:T(8,128)} %fusion.76, f32[1024,2048]{1,0:T(8,128)} %fusion.125, bf16[1024,2048]{0,1:T(8,128)(2,1)} %all-gather.23.cloned.1.call-done, ...), kind=kOutput, calls=%fused_computation.78 | convolution fusion | flops 8623489024 | bytes 50331648 | tf_op jit(solution)/shard_map/dot_general | solution.py:25
  935.2 140.7 %reduce-scatter.15.cloned.1.call-done = f32[256,2304]{0,1:T(8,128)} async-done(((f32[1024,2304]{0,1:T(8,128)}), f32[256,2304]{0,1:T(8,128)}) %reduce-scatter.15.cloned.1.call-update) | async-done | bytes 2359312 | tf_op jit(solution)/shard_map/reduce_scatter | solution.py:265
  1093.0 730.6 %while.29 = (s32[]{:T(128)}, f32[8,2,256,128]{3,2,1,0:T(8,128)}, f32[8,256,128]{2,1,0:T(8,128)}, bf16[8,256,128]{2,1,0:T(8,128)(2,1)}, bf16[8,2,256,128]{3,2,1,0...) while((s32[]{:T(128)}, f32[8,2,256,128]{3,2,1,0:T(8,128)}, ...), condition=%wide.region_14.15_spmd.clone, body=%wide.region_10.14_spmd.clone.sunk | while | flops 1361122304 | bytes 54558216 | solution.py:328
  1123.3 23.5 %reduce-scatter.33.cloned.1.call-done = bf16[256,128]{1,0:T(8,128)(2,1)} async-done(((bf16[2048,128]{1,0:T(8,128)(2,1)}), bf16[256,128]{1,0:T(8,128)(2,1)}) %reduce-scatter.33.cloned.1.call-update) | async-done | bytes 65552 | tf_op jit(solution)/shard_map/while/body/eval_jaxpr/reduce_scatter | solution.py:319
  1148.4 35.6 %reduce-scatter.35.cloned.1.call-done = bf16[256,128]{1,0:T(8,128)(2,1)} async-done(((bf16[2048,128]{1,0:T(8,128)(2,1)}), bf16[256,128]{1,0:T(8,128)(2,1)}) %reduce-scatter.35.cloned.1.call-update) | async-done | bytes 65552 | tf_op jit(solution)/shard_map/while/body/eval_jaxpr/reduce_scatter | solution.py:322
  1215.4 22.6 reduce-scatter.33.cloned.1.call-done
  1239.5 35.6 %reduce-scatter.35.cloned.1.call-done = bf16[256,128]{1,0:T(8,128)(2,1)} async-done(((bf16[2048,128]{1,0:T(8,128)(2,1)}), bf16[256,128]{1,0:T(8,128)(2,1)}) %reduce-scatter.35.cloned.1.call-update) | async-done | bytes 65552 | tf_op jit(solution)/shard_map/while/body/eval_jaxpr/reduce_scatter | solution.py:322
  1306.5 22.6 reduce-scatter.33.cloned.1.call-done
  1330.6 35.6 %reduce-scatter.35.cloned.1.call-done = bf16[256,128]{1,0:T(8,128)(2,1)} async-done(((bf16[2048,128]{1,0:T(8,128)(2,1)}), bf16[256,128]{1,0:T(8,128)(2,1)}) %reduce-scatter.35.cloned.1.call-update) | async-done | bytes 65552 | tf_op jit(solution)/shard_map/while/body/eval_jaxpr/reduce_scatter | solution.py:322
  1397.7 22.6 reduce-scatter.33.cloned.1.call-done
  1421.8 35.6 %reduce-scatter.35.cloned.1.call-done = bf16[256,128]{1,0:T(8,128)(2,1)} async-done(((bf16[2048,128]{1,0:T(8,128)(2,1)}), bf16[256,128]{1,0:T(8,128)(2,1)}) %reduce-scatter.35.cloned.1.call-update) | async-done | bytes 65552 | tf_op jit(solution)/shard_map/while/body/eval_jaxpr/reduce_scatter | solution.py:322
  1488.8 22.6 reduce-scatter.33.cloned.1.call-done
  1512.9 35.7 %reduce-scatter.35.cloned.1.call-done = bf16[256,128]{1,0:T(8,128)(2,1)} async-done(((bf16[2048,128]{1,0:T(8,128)(2,1)}), bf16[256,128]{1,0:T(8,128)(2,1)}) %reduce-scatter.35.cloned.1.call-update) | async-done | bytes 65552 | tf_op jit(solution)/shard_map/while/body/eval_jaxpr/reduce_scatter | solution.py:322
  1580.1 22.6 reduce-scatter.33.cloned.1.call-done
  1604.2 35.6 %reduce-scatter.35.cloned.1.call-done = bf16[256,128]{1,0:T(8,128)(2,1)} async-done(((bf16[2048,128]{1,0:T(8,128)(2,1)}), bf16[256,128]{1,0:T(8,128)(2,1)}) %reduce-scatter.35.cloned.1.call-update) | async-done | bytes 65552 | tf_op jit(solution)/shard_map/while/body/eval_jaxpr/reduce_scatter | solution.py:322
  1671.2 22.6 reduce-scatter.33.cloned.1.call-done
  1695.3 35.6 %reduce-scatter.35.cloned.1.call-done = bf16[256,128]{1,0:T(8,128)(2,1)} async-done(((bf16[2048,128]{1,0:T(8,128)(2,1)}), bf16[256,128]{1,0:T(8,128)(2,1)}) %reduce-scatter.35.cloned.1.call-update) | async-done | bytes 65552 | tf_op jit(solution)/shard_map/while/body/eval_jaxpr/reduce_scatter | solution.py:322
  1786.4 35.7 %reduce-scatter.35.cloned.1.call-done = bf16[256,128]{1,0:T(8,128)(2,1)} async-done(((bf16[2048,128]{1,0:T(8,128)(2,1)}), bf16[256,128]{1,0:T(8,128)(2,1)}) %reduce-scatter.35.cloned.1.call-update) | async-done | bytes 65552 | tf_op jit(solution)/shard_map/while/body/eval_jaxpr/reduce_scatter | solution.py:322
  1838.9 69.0 %reduce-scatter.13.cloned.1.call-done = bf16[256,2176]{0,1:T(8,128)(2,1)} async-done(((bf16[1024,2176]{0,1:T(8,128)(2,1)}), bf16[256,2176]{0,1:T(8,128)(2,1)}) %reduce-scatter.13.cloned.1.call-update) | async-done | bytes 1114128 | tf_op jit(solution)/shard_map/reduce_scatter | solution.py:238
  1957.0 75.5 %reduce-scatter.27.cloned.1.call-done = bf16[2,2,16,8192]{3,2,1,0:T(8,128)(2,1)} async-done(((bf16[8,2,16,8192]{3,2,1,0:T(8,128)(2,1)}), bf16[2,2,16,8192]{3,2,1,0:T(8,128)(2,1)}) %reduce-scatter.27.cloned.1.call-update) | async-done | bytes 1048592 | tf_op jit(solution)/shard_map/reduce_scatter | solution.py:405
  2032.5 24.7 %reduce-scatter.31.cloned.1.call-done = bf16[2,16,2048]{2,1,0:T(8,128)(2,1)} async-done(((bf16[8,16,2048]{2,1,0:T(8,128)(2,1)}), bf16[2,16,2048]{2,1,0:T(8,128)(2,1)}) %reduce-scatter.31.cloned.1.call-update) | async-done | bytes 131088 | tf_op jit(solution)/shard_map/reduce_scatter | solution.py:411
  2101.9 23.0 %reduce-scatter.17.cloned.1.call-done = bf16[2,16,2048]{2,1,0:T(8,128)(2,1)} async-done(((bf16[8,16,2048]{2,1,0:T(8,128)(2,1)}), bf16[2,16,2048]{2,1,0:T(8,128)(2,1)}) %reduce-scatter.17.cloned.1.call-update) | async-done | bytes 131088 | tf_op jit(solution)/shard_map/reduce_scatter | solution.py:390
  2124.9 27.7 %reduce-scatter.25.cloned.1.call-done = bf16[2,2,16,2048]{3,2,1,0:T(8,128)(2,1)} async-done(((bf16[8,2,16,2048]{3,2,1,0:T(8,128)(2,1)}), bf16[2,2,16,2048]{3,2,1,0:T(8,128)(2,1)}) %reduce-scatter.25.cloned.1.call-update) | async-done | bytes 262160 | tf_op jit(solution)/shard_map/reduce_scatter | solution.py:402
  2152.6 28.5 %reduce-scatter.19.cloned.1.call-done = bf16[2,16,4096]{2,1,0:T(8,128)(2,1)} async-done(((bf16[8,16,4096]{2,1,0:T(8,128)(2,1)}), bf16[2,16,4096]{2,1,0:T(8,128)(2,1)}) %reduce-scatter.19.cloned.1.call-update) | async-done | bytes 262160 | tf_op jit(solution)/shard_map/reduce_scatter | solution.py:393
  2193.3 56.1 %all-reduce.3.cloned.1.call-done = (bf16[2,16,2048]{2,1,0:T(8,128)(2,1)}, bf16[2,16,4096]{2,1,0:T(8,128)(2,1)}, bf16[2,16,2048]{2,1,0:T(8,128)(2,1)}, bf16[2,16,...) async-done(((bf16[2,16,2048]{2,1,0:T(8,128)(2,1)}, ...) | async-done | bytes 2621456 | tf_op jit(solution)/shard_map/psum | solution.py:417
  (505 shorter events, 845.1 us)
Async XLA Ops:
  7.2 123.3 %all-gather.15.cloned.1.call-start = ((), (), s32[]{:S(2)}) async-start(), calls=%async_computation.14 | async-start | bytes 17301504 | tf_op jit(solution)/shard_map/all_gather | solution.py:165
  7.9 150.4 %all-gather.13.cloned.1.call-start = ((), (), s32[]{:S(2)}) async-start(), calls=%async_computation.13 | async-start | bytes 1310720 | tf_op jit(solution)/shard_map/all_gather | solution.py:141
  8.7 209.4 %all-gather.17.cloned.1.call-start = ((), (), s32[]{:S(2)}) async-start(), calls=%async_computation.15 | async-start | bytes 4718592 | tf_op jit(solution)/shard_map/all_gather | solution.py:185
  174.7 75.1 %all-gather.19.cloned.1.call-start = ((), (), s32[]{:S(2)}) async-start(), calls=%async_computation.16 | async-start | bytes 4718592 | tf_op jit(solution)/shard_map/all_gather | solution.py:186
  179.0 150.7 %all-gather.21.cloned.1.call-start = ((), (), s32[]{:S(2)}) async-start(), calls=%async_computation.17 | async-start | bytes 8650752 | tf_op jit(solution)/shard_map/all_gather | solution.py:216
  179.6 354.9 %all-gather.27.cloned.1.call-start = ((), (), s32[]{:S(2)}) async-start(), calls=%async_computation.20 | async-start | bytes 1310720 | tf_op jit(solution)/shard_map/all_gather | solution.py:144
  180.2 355.7 %all-gather.31.cloned.1.call-start = ((), (), s32[]{:S(2)}) async-start(), calls=%async_computation.22 | async-start | bytes 2621440 | tf_op jit(solution)/shard_map/all_gather | solution.py:146
  180.9 363.8 %all-gather.29.cloned.1.call-start = ((), (), s32[]{:S(2)}) async-start(), calls=%async_computation.21 | async-start | bytes 5242880 | tf_op jit(solution)/shard_map/all_gather | solution.py:145
  181.7 449.2 %all-gather.23.cloned.1.call-start = ((), (), s32[]{:S(2)}) async-start(), calls=%async_computation.18 | async-start | bytes 5242880 | tf_op jit(solution)/shard_map/all_gather | solution.py:231
  339.9 415.3 %all-gather.25.cloned.1.call-start = ((), (), s32[]{:S(2)}) async-start(), calls=%async_computation.19 | async-start | bytes 28311552 | tf_op jit(solution)/shard_map/all_gather | solution.py:227
  492.1 345.4 %all-gather.33.cloned.1.call-start = ((), (), s32[]{:S(2)}) async-start(), calls=%async_computation.33 | async-start | bytes 5242880 | tf_op jit(solution)/shard_map/all_gather | solution.py:255
  492.9 583.0 %reduce-scatter.15.cloned.1.call-start = ((), (), s32[]{:S(2)}) async-start(), calls=%async_computation.24 | async-start | bytes 11796480 | tf_op jit(solution)/shard_map/reduce_scatter | solution.py:265
  1093.3 53.6 %reduce-scatter.33.cloned.1.call-start = ((), (), s32[]{:S(2)}) async-start(), calls=%async_computation.35 | async-start | bytes 589824 | tf_op jit(solution)/shard_map/while/body/eval_jaxpr/reduce_scatter | solution.py:319
  1111.6 72.3 %reduce-scatter.35.cloned.1.call-start = ((), (), s32[]{:S(2)}) async-start(), calls=%async_computation.36 | async-start | bytes 589824 | tf_op jit(solution)/shard_map/while/body/eval_jaxpr/reduce_scatter | solution.py:322
  1203.7 71.4 %reduce-scatter.35.cloned.1.call-start = ((), (), s32[]{:S(2)}) async-start(), calls=%async_computation.36 | async-start | bytes 589824 | tf_op jit(solution)/shard_map/while/body/eval_jaxpr/reduce_scatter | solution.py:322
  1294.8 71.4 %reduce-scatter.35.cloned.1.call-start = ((), (), s32[]{:S(2)}) async-start(), calls=%async_computation.36 | async-start | bytes 589824 | tf_op jit(solution)/shard_map/while/body/eval_jaxpr/reduce_scatter | solution.py:322
  1386.0 71.4 %reduce-scatter.35.cloned.1.call-start = ((), (), s32[]{:S(2)}) async-start(), calls=%async_computation.36 | async-start | bytes 589824 | tf_op jit(solution)/shard_map/while/body/eval_jaxpr/reduce_scatter | solution.py:322
  1477.1 71.5 %reduce-scatter.35.cloned.1.call-start = ((), (), s32[]{:S(2)}) async-start(), calls=%async_computation.36 | async-start | bytes 589824 | tf_op jit(solution)/shard_map/while/body/eval_jaxpr/reduce_scatter | solution.py:322
  1550.1 52.6 %reduce-scatter.33.cloned.1.call-start = ((), (), s32[]{:S(2)}) async-start(), calls=%async_computation.35 | async-start | bytes 589824 | tf_op jit(solution)/shard_map/while/body/eval_jaxpr/reduce_scatter | solution.py:319
  1568.4 71.4 %reduce-scatter.35.cloned.1.call-start = ((), (), s32[]{:S(2)}) async-start(), calls=%async_computation.36 | async-start | bytes 589824 | tf_op jit(solution)/shard_map/while/body/eval_jaxpr/reduce_scatter | solution.py:322
  1659.5 71.4 %reduce-scatter.35.cloned.1.call-start = ((), (), s32[]{:S(2)}) async-start(), calls=%async_computation.36 | async-start | bytes 589824 | tf_op jit(solution)/shard_map/while/body/eval_jaxpr/reduce_scatter | solution.py:322
  1750.7 71.5 %reduce-scatter.35.cloned.1.call-start = ((), (), s32[]{:S(2)}) async-start(), calls=%async_computation.36 | async-start | bytes 589824 | tf_op jit(solution)/shard_map/while/body/eval_jaxpr/reduce_scatter | solution.py:322
  1823.7 84.2 %reduce-scatter.13.cloned.1.call-start = ((), (), s32[]{:S(2)}) async-start(), calls=%async_computation.23 | async-start | bytes 5570560 | tf_op jit(solution)/shard_map/reduce_scatter | solution.py:238
  1824.4 132.6 %reduce-scatter.29.cloned.1.call-start = ((), (), s32[]{:S(2)}) async-start(), calls=%async_computation.31 | async-start | bytes 2621440 | tf_op jit(solution)/shard_map/reduce_scatter | solution.py:408
  1829.9 202.6 %reduce-scatter.27.cloned.1.call-start = ((), (), s32[]{:S(2)}) async-start(), calls=%async_computation.30 | async-start | bytes 5242880 | tf_op jit(solution)/shard_map/reduce_scatter | solution.py:405
  1838.9 218.3 %reduce-scatter.31.cloned.1.call-start = ((), (), s32[]{:S(2)}) async-start(), calls=%async_computation.32 | async-start | bytes 655360 | tf_op jit(solution)/shard_map/reduce_scatter | solution.py:411
  1910.6 168.9 %reduce-scatter.23.cloned.1.call-start = ((), (), s32[]{:S(2)}) async-start(), calls=%async_computation.28 | async-start | bytes 655360 | tf_op jit(solution)/shard_map/reduce_scatter | solution.py:399
  1913.6 188.3 %reduce-scatter.21.cloned.1.call-start = ((), (), s32[]{:S(2)}) async-start(), calls=%async_computation.27 | async-start | bytes 655360 | tf_op jit(solution)/shard_map/reduce_scatter | solution.py:396
  1921.0 203.9 %reduce-scatter.17.cloned.1.call-start = ((), (), s32[]{:S(2)}) async-start(), calls=%async_computation.25 | async-start | bytes 655360 | tf_op jit(solution)/shard_map/reduce_scatter | solution.py:390
  1939.2 213.3 %reduce-scatter.25.cloned.1.call-start = ((), (), s32[]{:S(2)}) async-start(), calls=%async_computation.29 | async-start | bytes 1310720 | tf_op jit(solution)/shard_map/reduce_scatter | solution.py:402
  1943.9 237.2 %reduce-scatter.19.cloned.1.call-start = ((), (), s32[]{:S(2)}) async-start(), calls=%async_computation.26 | async-start | bytes 1310720 | tf_op jit(solution)/shard_map/reduce_scatter | solution.py:393
  1951.5 298.0 %all-reduce.3.cloned.1.call-start = ((), (), s32[]{:S(2)}) async-start(), calls=%async_computation.34 | async-start | bytes 5242880 | tf_op jit(solution)/shard_map/psum | solution.py:417
  (99 other events, 4027.5 us)
Sparse Core Ops, SparseCore 0:
  11.0 119.4 all-gather.14
  132.1 26.1 all-gather.12
  174.8 35.9 all-gather.16
  213.1 36.5 all-gather.18
  252.5 77.1 all-gather.20
  331.1 26.5 all-gather.26
  359.3 91.2 all-gather.30
  452.2 92.4 all-gather.28
  546.9 83.9 all-gather.22
  632.7 122.4 all-gather.24
  756.8 80.7 all-gather.32
  916.1 159.6 reduce-scatter.14
  1111.8 35.0 reduce-scatter.32
  1149.8 34.1 reduce-scatter.34
  1203.8 34.1 reduce-scatter.32
  1240.9 34.1 reduce-scatter.34
  1295.0 34.1 reduce-scatter.32
  1332.1 34.1 reduce-scatter.34
  1386.1 34.1 reduce-scatter.32
  1423.2 34.1 reduce-scatter.34
  1477.2 34.1 reduce-scatter.32
  1514.4 34.1 reduce-scatter.34
  1568.5 34.1 reduce-scatter.32
  1605.6 34.1 reduce-scatter.34
  1659.6 34.1 reduce-scatter.32
  1696.7 34.1 reduce-scatter.34
  1750.8 34.1 reduce-scatter.32
  1788.0 34.1 reduce-scatter.34
  1826.8 81.0 reduce-scatter.12
  1910.0 44.0 reduce-scatter.28
  1956.5 75.9 reduce-scatter.26
  2185.1 64.2 all-reduce.2
  (6 shorter events, 133.6 us)
where the time goes:
time: 2280 us; the launch traced here: 2270 us
  waiting for transfers between devices  1380 us (61%)
  matrix products  447 us (20%)
  blocking collectives  228 us (10%)
  local copies, waits for them, and re-layouts  97.9 us (4%)
  other arithmetic  97.5 us (4%)
    reduce_scatter x8, waiting for transfers between devices, head_backward(): lax.psum_scatter(grad_value.astype(jnp.bfloat16), 'seq', scatter_dimensio...  285 us
    reduce_scatter x8, waiting for transfers between devices, head_backward(): lax.psum_scatter(grad_key.astype(jnp.bfloat16), 'seq', scatter_dimension=...  182 us
    reduce_scatter x1, waiting for transfers between devices, local(): lax.psum_scatter(jnp.concatenate([product_nt(d_gate, ffn_back[:, 0]) + pr...  141 us
    all_gather x1, waiting for transfers between devices, fetch_ffn(): return lax.all_gather(regrouped, 'seq', axis=0, tiled=True)  124 us
    all_to_all x1, blocking collectives, fetch_ffn(): lax.all_to_all(ffn, 'ad', split_axis=2, concat_axis=0, tiled=True)  116 us
    dot_general x15, matrix products, product(): return jnp.dot(matrix_a, matrix_b, preferred_element_type=jnp.float32)  101 us
    all_gather x1, waiting for transfers between devices, local(): lax.all_gather(wqkv, ('seq', 'ad'), axis=0, tiled=True)  96.2 us
    reduce_scatter x1, waiting for transfers between devices, local(): lax.psum_scatter(grad_terms[5].astype(jnp.bfloat16), 'ad', scatter_dimens...  75.5 us
  transfers between devices with their start and end apart: 38, of which 34 were waited for; matrix products, arithmetic and copies ran while one was open for 16% of the time, Pallas kernels for 0%

commit v1 on v0

v1 whole, which is shorter than its diff:
```python
import functools
import math

import jax
import jax.numpy as jnp
from jax import lax
from jax.experimental import pallas as pl
from jax.experimental.pallas import tpu as pltpu
from jax.sharding import PartitionSpec as P

QUERY_HEADS = 16
KEY_VALUE_HEADS = 8
HEADS_PER_GROUP = QUERY_HEADS // KEY_VALUE_HEADS
HEAD_SIZE = 128
FF = 8192
R = 16
NA = 8
PBLK = 8
CONTS = 8
BLOCK = 128
SLOTS = 16
GTOK = SLOTS * BLOCK
RANKS = NA * R

eps_norm = 1e-05
rope_base = 1000000.0
score_scale = 1.0 / math.sqrt(HEAD_SIZE)
NEG = -1e30
bf16 = jnp.bfloat16
f32 = jnp.float32


def nn(a, b):
    return jnp.dot(a, b, preferred_element_type=f32)


def nt(a, b):
    return lax.dot_general(a, b, (((1,), (1,)), ((), ())), preferred_element_type=f32)


def tn(a, b):
    return lax.dot_general(a, b, (((0,), (0,)), ((), ())), preferred_element_type=f32)


def norm_forward(values, gain):
    inverse = lax.rsqrt(jnp.mean(values * values, axis=-1, keepdims=True) + eps_norm)
    return (values * inverse * gain, inverse)


def norm_backward(values, inverse, gain, grads):
    weighted = grads * gain
    return inverse * weighted - values * (inverse * inverse * inverse) * jnp.mean(
        values * weighted, axis=-1, keepdims=True
    )


def rope_tables():
    half = HEAD_SIZE // 2
    frequency = jnp.exp(
        jnp.arange(half, dtype=f32) * (-2.0 * math.log(rope_base) / HEAD_SIZE)
    )
    position = jnp.arange((PBLK + 1) * BLOCK, dtype=f32)
    angles = position[:, None] * frequency[None, :]
    cosine, sine = jnp.cos(angles), jnp.sin(angles)
    return (
        jnp.concatenate([cosine, cosine], axis=1),
        jnp.concatenate([-sine, sine], axis=1),
    )


def select_matrix(role_row, owner_row):
    matches = (role_row - PBLK)[:, None] == jnp.arange(CONTS, dtype=jnp.int32)[None, :]
    owner_slot = jnp.max(jnp.where(matches, owner_row[None, :], -1), axis=1)
    owner_tok = jnp.repeat(owner_slot, BLOCK)
    column_owner = jnp.arange(RANKS, dtype=jnp.int32) // R
    return (owner_tok[:, None] == column_owner[None, :]).astype(f32)


def half_roll(x):
    return pltpu.roll(x, shift=HEAD_SIZE // 2, axis=1)


def causal_block(heads):
    rows = lax.broadcasted_iota(jnp.int32, (heads * BLOCK, BLOCK), 0) % BLOCK
    cols = lax.broadcasted_iota(jnp.int32, (heads * BLOCK, BLOCK), 1)
    return cols <= rows


def stack_heads(x):
    heads = x.shape[1] // HEAD_SIZE
    return jnp.concatenate(
        [x[:, j * HEAD_SIZE : (j + 1) * HEAD_SIZE] for j in range(heads)], axis=0
    )


def unstack_heads(x):
    heads = x.shape[0] // BLOCK
    return jnp.concatenate([x[j * BLOCK : (j + 1) * BLOCK] for j in range(heads)], axis=1)


def slot_rows(slot_ref, role):
    return pl.ds(pl.multiple_of(slot_ref[role] * BLOCK, BLOCK), BLOCK)


def role_rows(role):
    return pl.ds(pl.multiple_of(role * BLOCK, BLOCK), BLOCK)


def stack_rows(role, heads):
    n = heads * BLOCK
    return pl.ds(pl.multiple_of(role * n, n), n)


def attention_forward_kernel(slot_ref, proj_ref, cos_ref, sin_ref, attn_ref, qs_ref, kv_ref, lse_ref):
    heads = attn_ref.shape[1] // HEAD_SIZE
    qcols = heads * HEAD_SIZE

    def prepare(role, _):
        rows = slot_rows(slot_ref, role)
        table = role_rows(jnp.minimum(role, PBLK))
        cosine, sine = cos_ref[table, :], sin_ref[table, :]

        def turned(c):
            v = proj_ref[rows, c * HEAD_SIZE : (c + 1) * HEAD_SIZE]
            return (v * cosine + half_roll(v) * sine).astype(bf16)

        qs_ref[stack_rows(role, heads), :] = jnp.concatenate(
            [turned(j) for j in range(heads)], axis=0
        )
        kv_ref[role_rows(role), :HEAD_SIZE] = turned(heads)
        kv_ref[role_rows(role), HEAD_SIZE:] = proj_ref[rows, qcols + HEAD_SIZE :].astype(bf16)
        return 0

    lax.fori_loop(0, SLOTS, prepare, 0)
    causal = causal_block(heads)

    def one(role, prompt_blocks, own):
        q = qs_ref[stack_rows(role, heads), :]
        own_k = kv_ref[own, :HEAD_SIZE]
        own_v = kv_ref[own, HEAD_SIZE:]
        s_own = jnp.where(causal, nt(q, own_k) * score_scale, NEG)
        top = jnp.max(s_own, axis=1, keepdims=True)
        if prompt_blocks:
            n = prompt_blocks * BLOCK
            s_pre = nt(q, kv_ref[:n, :HEAD_SIZE]) * score_scale
            top = jnp.maximum(top, jnp.max(s_pre, axis=1, keepdims=True))
        e_own = jnp.exp(s_own - top)
        total = jnp.sum(e_own, axis=1, keepdims=True)
        out = nn(e_own.astype(bf16), own_v)
        if prompt_blocks:
            e_pre = jnp.exp(s_pre - top)
            total = total + jnp.sum(e_pre, axis=1, keepdims=True)
            out = out + nn(e_pre.astype(bf16), kv_ref[:n, HEAD_SIZE:])
        out = out / total
        lse_ref[stack_rows(role, heads), :] = top + jnp.log(total)
        attn_ref[slot_rows(slot_ref, role), :] = unstack_heads(out).astype(bf16)

    for role in range(PBLK):
        one(role, role, slice(role * BLOCK, (role + 1) * BLOCK))

    def later(c, _):
        one(PBLK + c, PBLK, role_rows(PBLK + c))
        return 0

    lax.fori_loop(0, CONTS, later, 0)


def attention_forward(slots, projected, cosine, sine):
    tokens = projected.shape[0]
    heads = projected.shape[1] // HEAD_SIZE - 2
    vm = pl.BlockSpec(memory_space=pltpu.VMEM)
    return pl.pallas_call(
        attention_forward_kernel,
        out_shape=(
            jax.ShapeDtypeStruct((tokens, heads * HEAD_SIZE), bf16),
            jax.ShapeDtypeStruct((tokens * heads, HEAD_SIZE), bf16),
            jax.ShapeDtypeStruct((tokens, 2 * HEAD_SIZE), bf16),
            jax.ShapeDtypeStruct((tokens * heads, 1), f32),
        ),
        in_specs=[pl.BlockSpec(memory_space=pltpu.SMEM), vm, vm, vm],
        out_specs=(vm, vm, vm, vm),
        cost_estimate=pl.CostEstimate(
            flops=4 * 10**9, bytes_accessed=10 * 2**20, transcendentals=4 * 10**6
        ),
        name="attention_forward",
    )(slots, projected, cosine, sine)


def attention_backward_kernel(
    slot_ref, qs_ref, kv_ref, lse_ref, grad_ref, cos_ref, sin_ref, out_ref, dk_ref, dv_ref
):
    heads = grad_ref.shape[1] // HEAD_SIZE
    qcols = heads * HEAD_SIZE
    dk_ref[...] = jnp.zeros_like(dk_ref)
    dv_ref[...] = jnp.zeros_like(dv_ref)
    causal = causal_block(heads)

    def turned_back(g, role):
        table = role_rows(jnp.minimum(role, PBLK))
        return g * cos_ref[table, :] - half_roll(g) * sin_ref[table, :]

    def one(role, prompt_blocks, own):
        q = qs_ref[stack_rows(role, heads), :]
        lse = lse_ref[stack_rows(role, heads), :]
        rows = slot_rows(slot_ref, role)
        g = stack_heads(grad_ref[rows, :])
        own_k = kv_ref[own, :HEAD_SIZE]
        own_v = kv_ref[own, HEAD_SIZE:]
        p_own = jnp.exp(jnp.where(causal, nt(q, own_k) * score_scale, NEG) - lse)
        dp_own = nt(g, own_v)
        centre = jnp.sum(p_own * dp_own, axis=1, keepdims=True)
        if prompt_blocks:
            n = prompt_blocks * BLOCK
            pre_k = kv_ref[:n, :HEAD_SIZE]
            p_pre = jnp.exp(nt(q, pre_k) * score_scale - lse)
            dp_pre = nt(g, kv_ref[:n, HEAD_SIZE:])
            centre = centre + jnp.sum(p_pre * dp_pre, axis=1, keepdims=True)
        ds_own = (p_own * (dp_own - centre) * score_scale).astype(bf16)
        dq = nn(ds_own, own_k)
        dk_ref[own, :] += tn(ds_own, q)
        dv_ref[own, :] += tn(p_own.astype(bf16), g)
        if prompt_blocks:
            ds_pre = (p_pre * (dp_pre - centre) * score_scale).astype(bf16)
            dq = dq + nn(ds_pre, pre_k)
            dk_ref[:n, :] += tn(ds_pre, q)
            dv_ref[:n, :] += tn(p_pre.astype(bf16), g)
        for j in range(heads):
            out_ref[rows, j * HEAD_SIZE : (j + 1) * HEAD_SIZE] = turned_back(
                dq[j * BLOCK : (j + 1) * BLOCK], role
            ).astype(bf16)

    for role in range(PBLK):
        one(role, role, slice(role * BLOCK, (role + 1) * BLOCK))

    def later(c, _):
        one(PBLK + c, PBLK, role_rows(PBLK + c))
        return 0

    lax.fori_loop(0, CONTS, later, 0)

    def finish(role, _):
        rows = slot_rows(slot_ref, role)
        out_ref[rows, qcols : qcols + HEAD_SIZE] = turned_back(dk_ref[role_rows(role), :], role).astype(bf16)
        out_ref[rows, qcols + HEAD_SIZE :] = dv_ref[role_rows(role), :].astype(bf16)
        return 0

    lax.fori_loop(0, SLOTS, finish, 0)


def attention_backward(slots, qs, kv, lse, grad, cosine, sine):
    tokens = kv.shape[0]
    vm = pl.BlockSpec(memory_space=pltpu.VMEM)
    return pl.pallas_call(
        attention_backward_kernel,
        out_shape=jax.ShapeDtypeStruct((tokens, grad.shape[1] + 2 * HEAD_SIZE), bf16),
        in_specs=[pl.BlockSpec(memory_space=pltpu.SMEM)] + [vm] * 6,
        out_specs=vm,
        scratch_shapes=[
            pltpu.VMEM((tokens, HEAD_SIZE), f32),
            pltpu.VMEM((tokens, HEAD_SIZE), f32),
        ],
        cost_estimate=pl.CostEstimate(
            flops=9 * 10**9, bytes_accessed=10 * 2**20, transcendentals=4 * 10**6
        ),
        name="attention_backward",
    )(slots, qs, kv, lse, grad, cosine, sine)


def gather_tokens(x):
    return lax.all_gather(x, "seq", axis=0, tiled=True)


def scatter_tokens(x):
    return lax.psum_scatter(x, "seq", scatter_dimension=0, tiled=True)


def head_columns(w, seq):
    split = seq // KEY_VALUE_HEADS
    if split == 1:
        return w
    rows, own = w.shape[0], HEADS_PER_GROUP // split
    w = w.reshape(rows, KEY_VALUE_HEADS, HEADS_PER_GROUP + 2, HEAD_SIZE)
    q = w[:, :, :HEADS_PER_GROUP].reshape(rows, KEY_VALUE_HEADS, split, own, HEAD_SIZE)
    kv = jnp.broadcast_to(
        w[:, :, None, HEADS_PER_GROUP:], (rows, KEY_VALUE_HEADS, split, 2, HEAD_SIZE)
    )
    return jnp.concatenate([q, kv], axis=3).reshape(rows, -1)


def joined_grad(g, seq):
    split = seq // KEY_VALUE_HEADS
    if split == 1:
        return g
    own = HEADS_PER_GROUP // split
    lead = g.shape[:-1]
    g = g.reshape(*lead, KEY_VALUE_HEADS, split, own + 2, HEAD_SIZE)
    q = g[..., :own, :].reshape(*lead, KEY_VALUE_HEADS, HEADS_PER_GROUP, HEAD_SIZE)
    return jnp.concatenate([q, jnp.sum(g[..., own:, :], axis=-3)], axis=-2).reshape(*lead, -1)


def column_shard(w):
    seq = lax.axis_size("seq")
    rows, columns = w.shape
    part = lax.all_to_all(w, "seq", split_axis=1, concat_axis=0, tiled=True)
    part = part.reshape(seq, rows, columns // seq)
    return lax.all_gather(part, "ad", axis=1, tiled=True).reshape(-1, columns // seq)


def local(
    tokens,
    out_grad,
    block_role,
    adapter_of,
    attn_gain,
    ffn_gain,
    wqkv,
    wo,
    ffn,
    qkv_a,
    qkv_b,
    out_a,
    out_b,
    ffn_in_a,
    ffn_in_b,
    ffn_out_a,
    ffn_out_b,
):
    own = tokens.shape[1]
    width = tokens.shape[2]
    seq = lax.axis_size("seq")
    rank_seq = lax.axis_index("seq")
    ff_part = FF // seq
    wqkv = head_columns(wqkv, seq)
    qkv_part = wqkv.shape[1] // seq
    head_part = QUERY_HEADS * HEAD_SIZE // seq
    row_start = rank_seq * own

    def my_columns(a, part):
        return lax.dynamic_slice_in_dim(a, rank_seq * part, part, a.ndim - 1)

    def stack_ad(a):
        return lax.all_gather(a, "ad", axis=0, tiled=True)

    role_row = block_role[0]
    slots = jnp.argsort(role_row).astype(jnp.int32)
    select_all = select_matrix(role_row, adapter_of[0])
    select_all_b = select_all.astype(bf16)
    select_own = lax.dynamic_slice_in_dim(select_all, row_start, own, 0)
    select_own_b = select_own.astype(bf16)
    cosine, sine = rope_tables()

    flat = lambda a: a.reshape(-1, a.shape[-1])
    first = stack_ad(jnp.concatenate([flat(qkv_a), my_columns(head_columns(flat(qkv_b), seq), qkv_part)], axis=1))
    qkv_enter, qkv_leave = first[:, :width], first[:, width:]
    second = stack_ad(
        jnp.concatenate(
            [
                flat(out_b),
                flat(ffn_in_a[:, 0]),
                flat(ffn_in_a[:, 1]),
                flat(ffn_out_b),
                my_columns(flat(out_a), head_part),
                my_columns(flat(ffn_in_b[:, 0]), ff_part),
                my_columns(flat(ffn_in_b[:, 1]), ff_part),
                my_columns(flat(ffn_out_a), ff_part),
            ],
            axis=1,
        )
    )
    cuts = [width] * 4 + [head_part] + [ff_part] * 3
    pieces, at = [], 0
    for c in cuts:
        pieces.append(second[:, at : at + c])
        at += c
    out_leave, gate_enter, upper_enter, down_leave, out_enter, gate_leave, upper_leave, down_enter = pieces

    qkv_w = column_shard(wqkv)
    out_w = lax.all_gather(wo, "ad", axis=0, tiled=True)
    w1 = column_shard(ffn[:, 0])
    w3 = column_shard(ffn[:, 1])
    w2 = column_shard(ffn[:, 2])

    inputs_f = tokens[0].astype(f32)
    normed, inverse_attn = norm_forward(inputs_f, attn_gain)
    normed_attn = normed.astype(bf16)
    normed_attn_all = gather_tokens(normed_attn)
    rank_qkv = nt(normed_attn_all, qkv_enter).astype(bf16) * select_all_b
    projected = nn(normed_attn_all, qkv_w) + nn(rank_qkv, qkv_leave)
    attn, qs, kv, lse = attention_forward(slots, projected, cosine, sine)
    branch = scatter_tokens(
        jnp.concatenate([nn(attn, out_w), nt(attn, out_enter)], axis=1).astype(bf16)
    )
    rank_out = branch[:, width:] * select_own_b
    residual = inputs_f + branch[:, :width].astype(f32) + nn(rank_out, out_leave)
    normed_two, inverse_ffn = norm_forward(residual, ffn_gain)
    normed_ffn = normed_two.astype(bf16)
    normed_ffn_all = gather_tokens(normed_ffn)
    rank_gate = nt(normed_ffn_all, gate_enter).astype(bf16) * select_all_b
    rank_upper = nt(normed_ffn_all, upper_enter).astype(bf16) * select_all_b
    gate_val = nn(normed_ffn_all, w1) + nn(rank_gate, gate_leave)
    upper_val = nn(normed_ffn_all, w3) + nn(rank_upper, upper_leave)
    sigma = jax.nn.sigmoid(gate_val)
    silu_gate = gate_val * sigma
    hidden = (silu_gate * upper_val).astype(bf16)
    down = scatter_tokens(
        jnp.concatenate([nt(hidden, w2), nt(hidden, down_enter)], axis=1).astype(bf16)
    )
    rank_down = down[:, width:] * select_own_b
    output = (
        residual + down[:, :width].astype(f32) + nn(rank_down, down_leave)
    ).astype(bf16)[None]

    grad_down = out_grad[0]
    grad_all = gather_tokens(grad_down)
    d_rank_down = (nt(grad_all, down_leave) * select_all).astype(bf16)
    d_hidden = nn(grad_all, w2) + nn(d_rank_down, down_enter)
    d_gate = (d_hidden * upper_val * sigma * (1.0 + gate_val * (1.0 - sigma))).astype(bf16)
    d_upper = (d_hidden * silu_gate).astype(bf16)
    back = scatter_tokens(
        jnp.concatenate(
            [
                nt(d_gate, w1) + nt(d_upper, w3),
                nt(d_gate, gate_leave),
                nt(d_upper, upper_leave),
            ],
            axis=1,
        ).astype(bf16)
    )
    d_rank_gate = back[:, width : width + RANKS] * select_own_b
    d_rank_upper = back[:, width + RANKS :] * select_own_b
    d_normed_ffn = (
        back[:, :width].astype(f32) + nn(d_rank_gate, gate_enter) + nn(d_rank_upper, upper_enter)
    )
    d_residual = grad_down.astype(f32) + norm_backward(
        residual, inverse_ffn, ffn_gain, d_normed_ffn
    )
    d_branch = d_residual.astype(bf16)
    d_branch_all = gather_tokens(d_branch)
    d_rank_out = (nt(d_branch_all, out_leave) * select_all).astype(bf16)
    d_attn = (nt(d_branch_all, out_w) + nn(d_rank_out, out_enter)).astype(bf16)
    d_projected = attention_backward(slots, qs, kv, lse, d_attn, cosine, sine)
    back_attn = scatter_tokens(
        jnp.concatenate([nt(d_projected, qkv_w), nt(d_projected, qkv_leave)], axis=1).astype(bf16)
    )
    d_rank_qkv = back_attn[:, width:] * select_own_b
    d_normed_attn = back_attn[:, :width].astype(f32) + nn(d_rank_qkv, qkv_enter)
    input_grad = (d_residual + norm_backward(inputs_f, inverse_attn, attn_gain, d_normed_attn))[
        None
    ]

    def reduced(partial, whole):
        cols = []
        if partial:
            part = width // seq
            stack = jnp.concatenate(
                [p.astype(bf16).reshape(RANKS, seq, part) for p in partial], axis=2
            ).transpose(1, 0, 2)
            cols.append(lax.psum_scatter(stack, "seq", scatter_dimension=0, tiled=True)[0])
        cols += [w.astype(bf16) for w in whole]
        both = jnp.concatenate(cols, axis=1)
        mine = lax.psum_scatter(both, "ad", scatter_dimension=0, tiled=True)
        return lax.all_gather(mine, "seq", axis=0)

    def unpack(arr, counts):
        out, at = [], 0
        for c in counts:
            piece = arr[:, :, at : at + c].transpose(1, 0, 2).astype(f32)
            out.append(piece.reshape(piece.shape[0] // R, R, seq * c))
            at += c
        return out

    wpart = width // seq
    early = reduced(
        [
            tn(rank_out, d_branch),
            tn(d_rank_gate, normed_ffn),
            tn(d_rank_upper, normed_ffn),
            tn(rank_down, grad_down),
        ],
        [
            tn(d_rank_out, attn),
            tn(rank_gate, d_gate),
            tn(rank_upper, d_upper),
            tn(d_rank_down, hidden),
        ],
    )
    g_out_b, g_ia0, g_ia1, g_ob, g_out_a, g_ib0, g_ib1, g_oa = unpack(
        early, [wpart] * 4 + [head_part] + [ff_part] * 3
    )
    late = reduced([tn(d_rank_qkv, normed_attn)], [tn(rank_qkv, d_projected)])
    g_qkv_a, g_qkv_b = unpack(late, [wpart, qkv_part])
    return (
        output,
        input_grad,
        g_qkv_a,
        joined_grad(g_qkv_b, seq),
        g_out_a,
        g_out_b,
        jnp.stack([g_ia0, g_ia1], axis=1),
        jnp.stack([g_ib0, g_ib1], axis=1),
        g_oa,
        g_ob,
    )


def solution(mesh):
    ad3 = P("ad", None, None)
    ad4 = P("ad", None, None, None)
    return jax.shard_map(
        local,
        mesh=mesh,
        in_specs=(
            P("ad", "seq", None),
            P("ad", "seq", None),
            P("ad", None),
            P("ad", None),
            P(),
            P(),
            P(("seq", "ad"), None),
            P(("seq", "ad"), None),
            P(("seq", "ad"), None, None),
            ad3,
            ad3,
            ad3,
            ad3,
            ad4,
            ad4,
            ad3,
            ad3,
        ),
        out_specs=(
            P("ad", "seq", None),
            P("ad", "seq", None),
            ad3,
            ad3,
            ad3,
            ad3,
            ad4,
            ad4,
            ad3,
            ad3,
        ),
        check_vma=False,
    )
```

time: 2280 us -> 1280 us (0.56)
  waiting for transfers between devices: 1380 us -> 781 us
  matrix products: 447 us -> 194 us
  blocking collectives: 228 us -> 117 us
  other arithmetic: 97.5 us -> 59 us
  local copies, waits for them, and re-layouts: 97.9 us -> 61 us
  Pallas kernels: 0 us -> 36.5 us
    reduce_scatter x26 -> x8, waiting for transfers between devices: 900 us -> 289 us  [the longest x4 185 us: scatter_tokens(): return lax.psum_scatter(x, 'seq', scatter_dimension=0, tiled=True)]
    dot_general x96 -> x40, matrix products: 447 us -> 194 us  [the longest x15 92.5 us: nt(): lax.dot_general(a, b, (((1,), (1,)), ((), ())), preferred_element_type=f32)]
    all_gather x6 -> x2, blocking collectives: 112 us -> 35.8 us  [the longest x1 26 us: stack_ad(): return lax.all_gather(a, 'ad', axis=0, tiled=True)]
    all_gather x11, waiting for transfers between devices: 414 us -> 490 us  [the longest x4 241 us: column_shard(): lax.all_gather(part, 'ad', axis=1, tiled=True).reshape(-1, columns // seq)]
    psum x1 -> x0, waiting for transfers between devices: 56.1 us -> none  [local(): lax.psum(shares[0].astype(jnp.bfloat16), 'seq').astype(jnp.float32)]
    pallas_call x0 -> x2, Pallas kernels: none -> 36.5 us  [the longest x1 21.2 us: attention_backward(): pl.pallas_call(attention_backward_kernel, out_shape=jax.ShapeDtypeStruct(...]
    all_to_all x1 -> x4, blocking collectives: 116 us -> 80.8 us  [column_shard(): part = lax.all_to_all(w, 'seq', split_axis=1, concat_axis=0, tiled=True)]
    unnamed x193 -> x131, local copies, waits for them, and re-layouts: 41.6 us -> 9.53 us
  transfers between devices with their start and end apart: 38 -> 19, of which waited for: 34 -> 18; matrix products, arithmetic and copies ran while one was open for 16% -> 15% of each run, Pallas kernels for 0% -> 3%
where the time goes in v1:
time: 1280 us; the launch traced here: 1270 us
  waiting for transfers between devices  781 us (61%)
  matrix products  194 us (15%)
  blocking collectives  117 us (9%)
  local copies, waits for them, and re-layouts  61 us (5%)
  other arithmetic  59 us (5%)
  Pallas kernels  36.5 us (3%)
  between operations  15.3 us (1%)
    all_gather x4, waiting for transfers between devices, column_shard(): lax.all_gather(part, 'ad', axis=1, tiled=True).reshape(-1, columns // seq)  241 us
    all_gather x4, waiting for transfers between devices, gather_tokens(): return lax.all_gather(x, 'seq', axis=0, tiled=True)  189 us
    reduce_scatter x4, waiting for transfers between devices, scatter_tokens(): return lax.psum_scatter(x, 'seq', scatter_dimension=0, tiled=True)  185 us
    dot_general x15, matrix products, nt(): lax.dot_general(a, b, (((1,), (1,)), ((), ())), preferred_element_type=f32)  92.5 us
    dot_general x15, matrix products, nn(): return jnp.dot(a, b, preferred_element_type=f32)  86.9 us
    all_to_all x4, blocking collectives, column_shard(): part = lax.all_to_all(w, 'seq', split_axis=1, concat_axis=0, tiled=True)  80.8 us
    reduce_scatter x2, waiting for transfers between devices, reduced(): lax.psum_scatter(stack, 'seq', scatter_dimension=0, tiled=True)[0]  58.5 us
    reduce_scatter x2, waiting for transfers between devices, reduced(): mine = lax.psum_scatter(both, 'ad', scatter_dimension=0, tiled=True)  45.8 us
  transfers between devices with their start and end apart: 19, of which 18 were waited for; matrix products, arithmetic and copies ran while one was open for 15% of the time, Pallas kernels for 3%

profile of v1, /device:TPU:0, one launch (start us, length us, event | category | flops | bytes accessed | tf_op | source)
XLA Modules:
  0.0 1265.1 jit_solution(4964821271375472033)
XLA Ops:
  8.5 14.8 %all_to_all.64 = bf16[64,8,512]{2,0,1:T(8,128)(2,1)S(1)} all-to-all(bf16[64,8,512]{2,0,1:T(8,128)(2,1)S(1)} %bitcast.196), channel_id=1, replica_groups=mesh['seq'=8,'ad'=4] {'seq'}, dimensions={1} | all-to-all | bytes 1048576 | tf_op jit(solution)/shard_map/all_to_all | solution.py:304
  32.2 26.0 %all_gather.47 = bf16[128,2560]{1,0:T(8,128)(2,1)S(1)} all-gather(bf16[32,2560]{1,0:T(8,128)(2,1)S(1)} %pad_maximum_fusion.7), channel_id=1, replica_groups=mesh['seq'=8,'ad'=4] {'ad'}, dimensions={0}, use_global_device_ids=true | all-gather | bytes 819200 | tf_op jit(solution)/shard_map/all_gather | solution.py:342
  65.2 15.0 %all-gather.17.cloned.1.call-done = bf16[8,256,512]{2,0,1:T(8,128)(2,1)} async-done(((bf16[8,64,512]{2,0,1:T(8,128)(2,1)}), bf16[8,256,512]{2,0,1:T(8,128)(2,1)}) %all-gather.17.cloned.1.call-update) | async-done | bytes 2097168 | tf_op jit(solution)/shard_map/all_gather | solution.py:306
  83.7 51.9 %all-gather.15.cloned.1.call-done = bf16[2048,2048]{1,0:T(8,128)(2,1)} async-done(((bf16[256,2048]{1,0:T(8,128)(2,1)}), bf16[2048,2048]{1,0:T(8,128)(2,1)}) %all-gather.15.cloned.1.call-update) | async-done | bytes 8388624 | tf_op jit(solution)/shard_map/all_gather | solution.py:270
  148.6 15.3 %attention_forward.1 = (bf16[2048,256]{1,0:T(8,128)(2,1)}, bf16[4096,128]{1,0:T(8,128)(2,1)}, bf16[2048,256]{1,0:T(8,128)(2,1)}, f32[4096,1]{1,0:T(8,128)}) custom-call(s32[16]{0:T(128)} %get-tuple-element.15.slot_ref, f32[2048,512]{1,0:T(8,128)} %convolution_add_fusion.3.proj_ref, f32[1152,128]{1,0:T(8,128)} %get-tuple-element.53.cos_ref, ...), custom_call_target="tpu_custom_call" | custom-call | flops 4000000000 | bytes 10485760 | tf_op jit(solution)/shard_map/attention_forward/pallas_call | solution.py:172
  163.9 33.5 %all-gather.21.cloned.1.call-done = bf16[128,11520]{1,0:T(8,128)(2,1)} async-done(((bf16[32,11520]{1,0:T(8,128)(2,1)}), bf16[128,11520]{1,0:T(8,128)(2,1)}) %all-gather.21.cloned.1.call-update) | async-done | bytes 2949136 | tf_op jit(solution)/shard_map/all_gather | solution.py:342
  199.1 26.5 %all-gather.19.cloned.1.call-done = bf16[256,2048]{1,0:T(8,128)(2,1)} async-done(((bf16[64,2048]{1,0:T(8,128)(2,1)}), bf16[256,2048]{1,0:T(8,128)(2,1)}) %all-gather.19.cloned.1.call-update) | async-done | bytes 1048592 | tf_op jit(solution)/shard_map/all_gather | solution.py:378
  244.1 18.8 %all_to_all.65 = bf16[64,8,1024]{2,0,1:T(8,128)(2,1)S(1)} all-to-all(bf16[64,8,1024]{2,0,1:T(8,128)(2,1)S(1)} %copy.152), channel_id=1, replica_groups=mesh['seq'=8,'ad'=4] {'seq'}, dimensions={1} | all-to-all | bytes 2097152 | tf_op jit(solution)/shard_map/all_to_all | solution.py:304
  265.7 29.4 %all_to_all.66 = bf16[64,8,1024]{2,0,1:T(8,128)(2,1)S(1)} all-to-all(bf16[64,8,1024]{2,0,1:T(8,128)(2,1)S(1)} %copy.158), channel_id=1, replica_groups=mesh['seq'=8,'ad'=4] {'seq'}, dimensions={1} | all-to-all | bytes 2097152 | tf_op jit(solution)/shard_map/all_to_all | solution.py:304
  297.9 17.8 %all_to_all.67 = bf16[64,8,1024]{2,0,1:T(8,128)(2,1)S(1)} all-to-all(bf16[64,8,1024]{2,0,1:T(8,128)(2,1)S(1)} %copy.155), channel_id=1, replica_groups=mesh['seq'=8,'ad'=4] {'seq'}, dimensions={1} | all-to-all | bytes 2097152 | tf_op jit(solution)/shard_map/all_to_all | solution.py:304
  318.4 10.5 reduce-scatter.9.cloned.1.call-done
  333.7 76.9 %all-gather.25.cloned.1.call-done = bf16[8,256,1024]{2,0,1:T(8,128)(2,1)} async-done(((bf16[8,64,1024]{2,0,1:T(8,128)(2,1)}), bf16[8,256,1024]{2,0,1:T(8,128)(2,1)}) %all-gather.25.cloned.1.call-update) | async-done | bytes 4194320 | tf_op jit(solution)/shard_map/all_gather | solution.py:306
  417.1 74.3 %all-gather.29.cloned.1.call-done = bf16[8,256,1024]{2,0,1:T(8,128)(2,1)} async-done(((bf16[8,64,1024]{2,0,1:T(8,128)(2,1)}), bf16[8,256,1024]{2,0,1:T(8,128)(2,1)}) %all-gather.29.cloned.1.call-update) | async-done | bytes 4194320 | tf_op jit(solution)/shard_map/all_gather | solution.py:306
  497.9 74.4 %all-gather.27.cloned.1.call-done = bf16[8,256,1024]{2,0,1:T(8,128)(2,1)} async-done(((bf16[8,64,1024]{2,0,1:T(8,128)(2,1)}), bf16[8,256,1024]{2,0,1:T(8,128)(2,1)}) %all-gather.27.cloned.1.call-update) | async-done | bytes 4194320 | tf_op jit(solution)/shard_map/all_gather | solution.py:306
  578.9 48.1 %all-gather.33.cloned.1.call-done = bf16[1,2048,2048]{2,1,0:T(8,128)(2,1)} async-done(((bf16[1,256,2048]{2,1,0:T(8,128)(2,1)}), bf16[1,2048,2048]{2,1,0:T(8,128)(2,1)}) %all-gather.33.cloned.1.call-update) | async-done | bytes 8388624 | tf_op jit(solution)/shard_map/all_gather | solution.py:270
  648.1 34.8 %all-gather.23.cloned.1.call-done = bf16[2048,2048]{1,0:T(8,128)(2,1)} async-done(((bf16[256,2048]{1,0:T(8,128)(2,1)}), bf16[2048,2048]{1,0:T(8,128)(2,1)}) %all-gather.23.cloned.1.call-update) | async-done | bytes 8388624 | tf_op jit(solution)/shard_map/all_gather | solution.py:270
  691.4 11.6 fusion.66
  703.0 13.3 %fusion.65 = f32[2048,1024]{1,0:T(8,128)} fusion(bf16[2048,2048]{1,0:T(8,128)(2,1)} %all-gather.23.cloned.1.call-done, bf16[2048,1024]{1,0:T(8,128)(2,1)S(1)} %bitcast.172), kind=kOutput, calls=%fused_computation.165 | convolution fusion | flops 8589934592 | bytes 20971520 | tf_op jit(solution)/shard_map/dot_general | solution.py:34
  721.0 11.3 multiply_convert_fusion.1
  732.3 14.7 %convolution_convert_fusion.1 = bf16[2048,2048]{1,0:T(8,128)(2,1)} fusion(bf16[2048,1024]{1,0:T(8,128)(2,1)} %get-tuple-element.24, bf16[2048,1024]{1,0:T(8,128)(2,1)} %bitcast.176), kind=kOutput, calls=%fused_computation.15 | convolution fusion | flops 8594128896 | bytes 16777216 | tf_op jit(solution)/shard_map/dot_general | solution.py:38
  764.8 12.1 fusion.67
  776.9 14.5 %add_convert_fusion = bf16[2048,2048]{1,0:T(8,128)(2,1)S(1)} fusion(f32[2048,2048]{1,0:T(8,128)} %fusion.67, bf16[2048,1024]{1,0:T(8,128)(2,1)} %get-tuple-element.23, bf16[2048,1024]{1,0:T(8,128)(2,1)} %bitcast.174), kind=kOutput, calls=%fused_computation | convolution fusion | flops 8598323200 | bytes 33554432 | tf_op jit(solution)/shard_map/dot_general | solution.py:38
  795.9 35.6 %reduce-scatter.11.cloned.1.call-done = bf16[256,2176]{1,0:T(8,128)(2,1)} async-done(((bf16[2048,2176]{1,0:T(8,128)(2,1)}), bf16[256,2176]{1,0:T(8,128)(2,1)}) %reduce-scatter.11.cloned.1.call-update) | async-done | bytes 1114128 | tf_op jit(solution)/shard_map/reduce_scatter | solution.py:274
  833.6 78.2 %reduce-scatter.13.cloned.1.call-done = bf16[256,2304]{1,0:T(8,128)(2,1)} async-done(((bf16[2048,2304]{1,0:T(8,128)(2,1)}), bf16[256,2304]{1,0:T(8,128)(2,1)}) %reduce-scatter.13.cloned.1.call-update) | async-done | bytes 1179664 | tf_op jit(solution)/shard_map/reduce_scatter | solution.py:274
  926.7 40.4 %reduce-scatter.21.cloned.1.call-done = bf16[1,128,1024]{2,1,0:T(8,128)(2,1)} async-done(((bf16[8,128,1024]{2,1,0:T(8,128)(2,1)}), bf16[1,128,1024]{2,1,0:T(8,128)(2,1)}) %reduce-scatter.21.cloned.1.call-update) | async-done | bytes 262160 | tf_op jit(solution)/shard_map/reduce_scatter | solution.py:458
  968.8 54.3 %all-gather.31.cloned.1.call-done = bf16[2048,2048]{1,0:T(8,128)(2,1)} async-done(((bf16[256,2048]{1,0:T(8,128)(2,1)}), bf16[2048,2048]{1,0:T(8,128)(2,1)}) %all-gather.31.cloned.1.call-update) | async-done | bytes 8388624 | tf_op jit(solution)/shard_map/all_gather | solution.py:270
  1035.0 28.4 %reduce-scatter.23.cloned.1.call-done = bf16[32,4352]{1,0:T(8,128)(2,1)} async-done(((bf16[128,4352]{1,0:T(8,128)(2,1)}), bf16[32,4352]{1,0:T(8,128)(2,1)}) %reduce-scatter.23.cloned.1.call-update) | async-done | bytes 278544 | tf_op jit(solution)/shard_map/reduce_scatter | solution.py:461
  1071.9 21.2 %attention_backward.1 = bf16[2048,512]{1,0:T(8,128)(2,1)} custom-call(s32[16]{0:T(128)} %get-tuple-element.15.slot_ref, bf16[4096,128]{1,0:T(8,128)(2,1)} %get-tuple-element.17.qs_ref, bf16[2048,256]{1,0:T(8,128)(2,1)} %get-tuple-element.18.kv_ref, f32[4096,1]{1,0:T(8,128)} %get-tuple-element.19.lse_ref, bf16[2048,256]{1,0:T(8,128)(2,1)} %fusion.8.grad_ref, ...), custom_call_target="tpu_custom_call" | custom-call | flops 8999999488 | bytes 10485760 | tf_op jit(solution)/shard_map/attention_backward/pallas_call | solution.py:253
  1095.4 10.1 convolution_convert_fusion
  1125.7 60.9 %reduce-scatter.15.cloned.1.call-done = bf16[256,2176]{1,0:T(8,128)(2,1)} async-done(((bf16[2048,2176]{1,0:T(8,128)(2,1)}), bf16[256,2176]{1,0:T(8,128)(2,1)}) %reduce-scatter.15.cloned.1.call-update) | async-done | bytes 1114128 | tf_op jit(solution)/shard_map/reduce_scatter | solution.py:274
  1205.6 18.1 %reduce-scatter.17.cloned.1.call-done = bf16[1,128,256]{2,1,0:T(8,128)(2,1)} async-done(((bf16[8,128,256]{2,1,0:T(8,128)(2,1)}), bf16[1,128,256]{2,1,0:T(8,128)(2,1)}) %reduce-scatter.17.cloned.1.call-update) | async-done | bytes 65552 | tf_op jit(solution)/shard_map/reduce_scatter | solution.py:458
  1228.7 17.4 %reduce-scatter.19.cloned.1.call-done = bf16[32,768]{1,0:T(8,128)(2,1)} async-done(((bf16[128,768]{1,0:T(8,128)(2,1)}), bf16[32,768]{1,0:T(8,128)(2,1)}) %reduce-scatter.19.cloned.1.call-update) | async-done | bytes 49168 | tf_op jit(solution)/shard_map/reduce_scatter | solution.py:461
  (279 shorter events, 239.5 us)
Async XLA Ops:
  7.2 72.9 %all-gather.17.cloned.1.call-start = ((), (), s32[]{:S(2)}) async-start(), calls=%async_computation.13 | async-start | bytes 2621440 | tf_op jit(solution)/shard_map/all_gather | solution.py:306
  24.4 111.2 %all-gather.15.cloned.1.call-start = ((), (), s32[]{:S(2)}) async-start(), calls=%async_computation.12 | async-start | bytes 9437184 | tf_op jit(solution)/shard_map/all_gather | solution.py:270
  26.7 170.7 %all-gather.21.cloned.1.call-start = ((), (), s32[]{:S(2)}) async-start(), calls=%async_computation.15 | async-start | bytes 3686400 | tf_op jit(solution)/shard_map/all_gather | solution.py:342
  30.4 195.1 %all-gather.19.cloned.1.call-start = ((), (), s32[]{:S(2)}) async-start(), calls=%async_computation.14 | async-start | bytes 1310720 | tf_op jit(solution)/shard_map/all_gather | solution.py:378
  31.0 297.9 %reduce-scatter.9.cloned.1.call-start = ((), (), s32[]{:S(2)}) async-start(), calls=%async_computation.16 | async-start | bytes 10027008 | tf_op jit(solution)/shard_map/reduce_scatter | solution.py:274
  58.2 87.7 %copy-start.27 = (bf16[128,2560]{1,0:T(8,128)(2,1)}, bf16[128,2560]{1,0:T(8,128)(2,1)S(1)}, u32[]{:S(2)}) copy-start(bf16[128,2560]{1,0:T(8,128)(2,1)S(1)} %all_gather.47) | copy-start | bytes 1966084
  240.7 169.9 %all-gather.25.cloned.1.call-start = ((), (), s32[]{:S(2)}) async-start(), calls=%async_computation.18 | async-start | bytes 5242880 | tf_op jit(solution)/shard_map/all_gather | solution.py:306
  264.5 227.0 %all-gather.29.cloned.1.call-start = ((), (), s32[]{:S(2)}) async-start(), calls=%async_computation.20 | async-start | bytes 5242880 | tf_op jit(solution)/shard_map/all_gather | solution.py:306
  296.7 275.6 %all-gather.27.cloned.1.call-start = ((), (), s32[]{:S(2)}) async-start(), calls=%async_computation.19 | async-start | bytes 5242880 | tf_op jit(solution)/shard_map/all_gather | solution.py:306
  317.3 309.7 %all-gather.33.cloned.1.call-start = ((), (), s32[]{:S(2)}) async-start(), calls=%async_computation.29 | async-start | bytes 9437184 | tf_op jit(solution)/shard_map/all_gather | solution.py:270
  318.0 365.0 %all-gather.23.cloned.1.call-start = ((), (), s32[]{:S(2)}) async-start(), calls=%async_computation.17 | async-start | bytes 9437184 | tf_op jit(solution)/shard_map/all_gather | solution.py:270
  318.4 98.7 %copy-start.28 = (bf16[2048,128]{1,0:T(8,128)(2,1)}, bf16[2048,128]{1,0:T(8,128)(2,1)S(1)}, u32[]{:S(2)}) copy-start(bf16[2048,128]{1,0:T(8,128)(2,1)S(1)} %compare_convert_fusion) | copy-start | bytes 1572868
  331.5 85.6 %copy-start.50 = (f32[256]{0:T(256)}, f32[256]{0:T(256)S(1)}, u32[]{:S(2)}) copy-start(f32[256]{0:T(256)S(1)} %get-tuple-element.43) | copy-start | bytes 3076
  333.5 498.0 %reduce-scatter.11.cloned.1.call-start = ((), (), s32[]{:S(2)}) async-start(), calls=%async_computation.21 | async-start | bytes 10027008 | tf_op jit(solution)/shard_map/reduce_scatter | solution.py:274
  497.9 129.1 %copy-start.16 = (bf16[128,11520]{1,0:T(8,128)(2,1)S(1)}, bf16[128,11520]{1,0:T(8,128)(2,1)}, u32[]{:S(2)}) copy-start(bf16[128,11520]{1,0:T(8,128)(2,1)} %all-gather.21.cloned.1.call-done) | copy-start | bytes 8847364
  757.2 154.5 %reduce-scatter.13.cloned.1.call-start = ((), (), s32[]{:S(2)}) async-start(), calls=%async_computation.22 | async-start | bytes 10616832 | tf_op jit(solution)/shard_map/reduce_scatter | solution.py:274
  795.8 35.7 %copy-start.9 = (bf16[1,256,2048]{2,1,0:T(8,128)(2,1)S(1)}, bf16[1,256,2048]{2,1,0:T(8,128)(2,1)}, u32[]{:S(2)}) copy-start(bf16[1,256,2048]{2,1,0:T(8,128)(2,1)} %param.18) | copy-start | bytes 3145732
  795.8 115.9 %copy-start.7 = (bf16[256,2048]{1,0:T(8,128)(2,1)S(1)}, bf16[256,2048]{1,0:T(8,128)(2,1)}, u32[]{:S(2)}) copy-start(bf16[256,2048]{1,0:T(8,128)(2,1)} %multiply_convert_fusion.3) | copy-start | bytes 3145732
  795.9 171.3 %reduce-scatter.21.cloned.1.call-start = ((), (), s32[]{:S(2)}) async-start(), calls=%async_computation.27 | async-start | bytes 2359296 | tf_op jit(solution)/shard_map/reduce_scatter | solution.py:458
  833.6 84.2 %copy-start.3 = (f32[256,2048]{1,0:T(8,128)S(1)}, f32[256,2048]{1,0:T(8,128)}, u32[]{:S(2)}) copy-start(f32[256,2048]{1,0:T(8,128)} %copy-done.2) | copy-start | bytes 6291460
  833.6 84.2 %copy-start.45 = (f32[2048]{0:T(1024)S(1)}, f32[2048]{0:T(1024)}, u32[]{:S(2)}) copy-start(f32[2048]{0:T(1024)} %param.22) | copy-start | bytes 24580
  925.9 97.3 %all-gather.31.cloned.1.call-start = ((), (), s32[]{:S(2)}) async-start(), calls=%async_computation.23 | async-start | bytes 9437184 | tf_op jit(solution)/shard_map/all_gather | solution.py:270
  926.5 136.9 %reduce-scatter.23.cloned.1.call-start = ((), (), s32[]{:S(2)}) async-start(), calls=%async_computation.28 | async-start | bytes 1392640 | tf_op jit(solution)/shard_map/reduce_scatter | solution.py:461
  968.8 60.3 %copy-start.8 = (bf16[2048,256]{1,0:T(8,128)(2,1)S(1)}, bf16[2048,256]{1,0:T(8,128)(2,1)}, u32[]{:S(2)}) copy-start(bf16[2048,256]{1,0:T(8,128)(2,1)} %get-tuple-element.16) | copy-start | bytes 3145732
  1034.9 84.4 %all-gather.35.cloned.1.call-start = ((), (), s32[]{:S(2)}) async-start(), calls=%async_computation.30 | async-start | bytes 2506752 | tf_op jit(solution)/shard_map/all_gather | solution.py:462
  1063.4 123.1 %reduce-scatter.15.cloned.1.call-start = ((), (), s32[]{:S(2)}) async-start(), calls=%async_computation.24 | async-start | bytes 10027008 | tf_op jit(solution)/shard_map/reduce_scatter | solution.py:274
  1113.5 110.2 %reduce-scatter.17.cloned.1.call-start = ((), (), s32[]{:S(2)}) async-start(), calls=%async_computation.25 | async-start | bytes 589824 | tf_op jit(solution)/shard_map/reduce_scatter | solution.py:458
  1121.2 65.4 %copy-start.12 = (bf16[256,2048]{1,0:T(8,128)(2,1)S(1)}, bf16[256,2048]{1,0:T(8,128)(2,1)}, u32[]{:S(2)}) copy-start(bf16[256,2048]{1,0:T(8,128)(2,1)} %fusion.25) | copy-start | bytes 3145732
  1188.7 57.5 %reduce-scatter.19.cloned.1.call-start = ((), (), s32[]{:S(2)}) async-start(), calls=%async_computation.26 | async-start | bytes 245760 | tf_op jit(solution)/shard_map/reduce_scatter | solution.py:461
  1194.7 30.5 %copy-start.49 = (f32[256]{0:T(256)S(1)}, f32[256]{0:T(256)}, u32[]{:S(2)}) copy-start(f32[256]{0:T(256)} %copy-done.48) | copy-start | bytes 3076
  1194.7 30.5 %copy-start.52 = (f32[256]{0:T(256)S(1)}, f32[256]{0:T(256)}, u32[]{:S(2)}) copy-start(f32[256]{0:T(256)} %get-tuple-element.40) | copy-start | bytes 3076
  1225.2 32.9 %copy-start.1 = (bf16[2,16,4096]{2,1,0:T(8,128)(2,1)S(1)}, bf16[2,16,4096]{2,1,0:T(8,128)(2,1)}, u32[]{:S(2)}) copy-start(bf16[2,16,4096]{2,1,0:T(8,128)(2,1)} %param.27) | copy-start | bytes 786436
  (47 other events, 498.2 us)
Sparse Core Ops, SparseCore 0:
  24.6 55.5 all-gather.16
  82.6 52.9 all-gather.14
  137.2 60.1 all-gather.20
  198.9 26.6 all-gather.18
  240.9 87.9 reduce-scatter.8
  330.3 80.2 all-gather.24
  412.2 79.2 all-gather.28
  493.0 79.2 all-gather.26
  574.2 52.7 all-gather.32
  628.7 54.2 all-gather.22
  757.3 74.1 reduce-scatter.10
  834.9 76.8 reduce-scatter.12
  926.0 41.0 reduce-scatter.20
  968.9 54.2 all-gather.30
  1035.1 28.2 reduce-scatter.22
  1065.1 26.8 all-gather.34
  1113.6 72.9 reduce-scatter.14
  1189.5 34.0 reduce-scatter.16
  1226.5 19.6 reduce-scatter.18

commit v2 on v1

--- a/solution.py
+++ b/solution.py
@@ -266,12 +266,236 @@
     )(slots, qs, kv, lse, grad, cosine, sine)
 
 
+PLANE = 8
+
+
+def neighbours():
+    me = lax.axis_index("seq")
+    core, x, y = me % 2, (me // 2) % 2, me // 4
+    p = me + 1 - 2 * core
+    nx = me + 2 - 4 * x
+    ny = me + 4 - 8 * y
+    nd = nx + 4 - 8 * y
+    return me, p, nx, ny, nd
+
+
+def across(i):
+    return i + 1 - 2 * (i % 2)
+
+
+def greet(*others):
+    barrier = pltpu.get_barrier_semaphore()
+    for other in others:
+        pl.semaphore_signal(
+            barrier, inc=1, device_id={"seq": other}, device_id_type=pl.DeviceIdType.MESH
+        )
+    pl.semaphore_wait(barrier, len(others))
+
+
+class Links:
+    def __init__(self, send_sem, recv_sem):
+        self.send_sem, self.recv_sem, self.made = send_sem, recv_sem, {}
+
+    def start(self, k, src, dst, to):
+        copy = pltpu.make_async_remote_copy(
+            src_ref=src,
+            dst_ref=dst,
+            send_sem=self.send_sem.at[k],
+            recv_sem=self.recv_sem.at[k],
+            device_id={"seq": to},
+            device_id_type=pl.DeviceIdType.MESH,
+        )
+        copy.start()
+        self.made[k] = copy
+
+    def arrived(self, k):
+        self.made[k].wait_recv()
+
+    def drain(self):
+        for copy in self.made.values():
+            copy.wait_send()
+
+
+def gather_kernel(own_ref, all_ref, send_sem, recv_sem):
+    own = own_ref.shape[0]
+    half = own // 2
+    me, p, nx, ny, nd = neighbours()
+    greet(p, nx, ny)
+    links = Links(send_sem, recv_sem)
+
+    def piece(i, h):
+        return all_ref.at[pl.ds(pl.multiple_of(i * own + h * half, half), half), :]
+
+    mine = own_ref.at
+    links.start(0, mine[:half, :], piece(me, 0), nx)
+    links.start(1, mine[half:, :], piece(me, 1), ny)
+    links.start(2, mine[half:, :], piece(me, 1), nx)
+    links.start(3, mine[:half, :], piece(me, 0), ny)
+    block = all_ref.at[pl.ds(pl.multiple_of(me * own, own), own), :]
+    links.start(4, own_ref, block, p)
+    all_ref[pl.ds(pl.multiple_of(me * own, own), own), :] = own_ref[...]
+
+    links.arrived(0)
+    links.start(5, piece(nx, 0), piece(nx, 0), ny)
+    links.start(7, piece(nx, 0), piece(nx, 0), p)
+    links.arrived(1)
+    links.start(6, piece(ny, 1), piece(ny, 1), nx)
+    links.start(8, piece(ny, 1), piece(ny, 1), p)
+    links.arrived(2)
+    links.start(9, piece(nx, 1), piece(nx, 1), p)
+    links.arrived(3)
+    links.start(10, piece(ny, 0), piece(ny, 0), p)
+    links.arrived(5)
+    links.start(11, piece(nd, 0), piece(nd, 0), p)
+    links.arrived(6)
+    links.start(12, piece(nd, 1), piece(nd, 1), p)
+    for k in (4, 7, 8, 9, 10, 11, 12):
+        links.arrived(k)
+    links.drain()
+
+
 def gather_tokens(x):
-    return lax.all_gather(x, "seq", axis=0, tiled=True)
-
-
-def scatter_tokens(x):
-    return lax.psum_scatter(x, "seq", scatter_dimension=0, tiled=True)
+    if lax.axis_size("seq") != PLANE:
+        return lax.all_gather(x, "seq", axis=0, tiled=True)
+    own, width = x.shape
+    vm = pl.BlockSpec(memory_space=pltpu.VMEM)
+    return pl.pallas_call(
+        gather_kernel,
+        out_shape=jax.ShapeDtypeStruct((PLANE * own, width), x.dtype),
+        in_specs=[vm],
+        out_specs=vm,
+        scratch_shapes=[pltpu.SemaphoreType.DMA((13,)), pltpu.SemaphoreType.DMA((13,))],
+        compiler_params=pltpu.CompilerParams(collective_id=1, has_side_effects=True),
+        cost_estimate=pl.CostEstimate(
+            flops=0, bytes_accessed=10 * PLANE * own * width, transcendentals=0
+        ),
+        name="gather_tokens",
+    )(x)
+
+
+COLS = 256
+
+
+def scatter_kernel(modes, *refs):
+    n = len(modes)
+    a_refs, b_refs, r_refs = refs[:n], refs[n : 2 * n], refs[2 * n : 3 * n]
+    out_ref, rank_ref, theirs, cores, sums, relay, last, send_sem, recv_sem = refs[3 * n :]
+    own, width = out_ref.shape
+    ranks = rank_ref.shape[1]
+    half = own // 2
+    per = ranks // n
+    me, p, nx, ny, nd = neighbours()
+    greet(p, nx, ny)
+    links = Links(send_sem, recv_sem)
+
+    def product(i, store):
+        rows = pl.ds(pl.multiple_of(i * own, own), own)
+
+        def tile(t, _):
+            cols = pl.ds(pl.multiple_of(t * COLS, COLS), COLS)
+            total = None
+            for a, b, transposed in zip(a_refs, b_refs, modes):
+                term = nt(a[rows, :], b[cols, :]) if transposed else nn(a[rows, :], b[:, cols])
+                total = term if total is None else total + term
+            store(cols, total)
+            return 0
+
+        lax.fori_loop(0, width // COLS, tile, 0)
+        for j, (a, r) in enumerate(zip(a_refs, r_refs)):
+            store(slice(width + j * per, width + (j + 1) * per), nt(a[rows, :], r[...]))
+
+    def for_partner(slot, i):
+        def store(cols, value):
+            theirs[slot, :, cols] = value.astype(bf16)
+
+        product(across(i), store)
+        links.start(slot, theirs.at[slot], cores.at[slot], p)
+
+    def chip_sum(slot, i):
+        def store(cols, value):
+            sums[slot, :, cols] = (value + cores[slot, :, cols].astype(f32)).astype(bf16)
+
+        product(i, store)
+
+    for_partner(0, nd)
+    for_partner(1, nx)
+    links.arrived(0)
+    chip_sum(0, nd)
+    links.start(4, sums.at[0, :half], relay.at[0], nx)
+    links.start(5, sums.at[0, half:], relay.at[1], ny)
+    links.arrived(1)
+    chip_sum(1, nx)
+    links.start(6, sums.at[1, :half], last.at[0, :half], nx)
+    for_partner(2, ny)
+    for_partner(3, me)
+    links.arrived(2)
+    chip_sum(2, ny)
+    links.start(7, sums.at[2, half:], last.at[1, half:], ny)
+    links.arrived(5)
+    sums[1, half:, :] = (sums[1, half:, :].astype(f32) + relay[1].astype(f32)).astype(bf16)
+    links.start(8, sums.at[1, half:], last.at[0, half:], nx)
+    links.arrived(4)
+    sums[2, :half, :] = (sums[2, :half, :].astype(f32) + relay[0].astype(f32)).astype(bf16)
+    links.start(9, sums.at[2, :half], last.at[1, :half], ny)
+    links.arrived(3)
+
+    def keep(cols, value):
+        value = value + cores[3, :, cols].astype(f32)
+        if isinstance(cols, slice):
+            rank_ref[:, cols.start - width : cols.stop - width] = value
+        else:
+            out_ref[:, cols] = value
+
+    product(me, keep)
+    for k in (6, 7, 8, 9):
+        links.arrived(k)
+    both = lambda cols: last[0, :, cols].astype(f32) + last[1, :, cols].astype(f32)
+    out_ref[...] = out_ref[...] + both(slice(0, width))
+    rank_ref[...] = rank_ref[...] + both(slice(width, width + ranks))
+    links.drain()
+
+
+def scatter_products(terms, collective_id):
+    modes = tuple(t[3] for t in terms)
+    a, b, r = ([t[k] for t in terms] for k in range(3))
+    width = b[0].shape[0] if modes[0] else b[0].shape[1]
+    ranks = sum(x.shape[0] for x in r)
+    seq = lax.axis_size("seq")
+    rows = a[0].shape[0]
+    own = rows // seq
+    if seq != PLANE:
+        total = sum(nt(x, y) if m else nn(x, y) for x, y, m in zip(a, b, modes))
+        both = jnp.concatenate([total] + [nt(x, y) for x, y in zip(a, r)], axis=1).astype(bf16)
+        both = lax.psum_scatter(both, "seq", scatter_dimension=0, tiled=True).astype(f32)
+        return both[:, :width], both[:, width:]
+    vm = pl.BlockSpec(memory_space=pltpu.VMEM)
+    whole = width + ranks
+    depth = sum(x.shape[1] for x in a)
+    return pl.pallas_call(
+        functools.partial(scatter_kernel, modes),
+        out_shape=(
+            jax.ShapeDtypeStruct((own, width), f32),
+            jax.ShapeDtypeStruct((own, ranks), f32),
+        ),
+        in_specs=[vm] * (3 * len(terms)),
+        out_specs=(vm, vm),
+        scratch_shapes=[
+            pltpu.VMEM((4, own, whole), bf16),
+            pltpu.VMEM((4, own, whole), bf16),
+            pltpu.VMEM((3, own, whole), bf16),
+            pltpu.VMEM((2, own // 2, whole), bf16),
+            pltpu.VMEM((2, own, whole), bf16),
+            pltpu.SemaphoreType.DMA((10,)),
+            pltpu.SemaphoreType.DMA((10,)),
+        ],
+        compiler_params=pltpu.CompilerParams(collective_id=collective_id, has_side_effects=True),
+        cost_estimate=pl.CostEstimate(
+            flops=2 * rows * depth * whole + 4 * 10**10,
+            bytes_accessed=rows * depth * 4,
+            transcendentals=0,
+        ),
+        name=f"scatter_products_{collective_id}",
+    )(*a, *b, *r)
 
 
 def head_columns(w, seq):
@@ -387,11 +611,9 @@
     rank_qkv = nt(normed_attn_all, qkv_enter).astype(bf16) * select_all_b
     projected = nn(normed_attn_all, qkv_w) + nn(rank_qkv, qkv_leave)
     attn, qs, kv, lse = attention_forward(slots, projected, cosine, sine)
-    branch = scatter_tokens(
-        jnp.concatenate([nn(attn, out_w), nt(attn, out_enter)], axis=1).astype(bf16)
-    )
-    rank_out = branch[:, width:] * select_own_b
-    residual = inputs_f + branch[:, :width].astype(f32) + nn(rank_out, out_leave)
+    branch, rank_out = scatter_products([(attn, out_w, out_enter, False)], 2)
+    rank_out = rank_out.astype(bf16) * select_own_b
+    residual = inputs_f + branch + nn(rank_out, out_leave)
     normed_two, inverse_ffn = norm_forward(residual, ffn_gain)
     normed_ffn = normed_two.astype(bf16)
     normed_ffn_all = gather_tokens(normed_ffn)
@@ -402,13 +624,9 @@
     sigma = jax.nn.sigmoid(gate_val)
     silu_gate = gate_val * sigma
     hidden = (silu_gate * upper_val).astype(bf16)
-    down = scatter_tokens(
-        jnp.concatenate([nt(hidden, w2), nt(hidden, down_enter)], axis=1).astype(bf16)
-    )
-    rank_down = down[:, width:] * select_own_b
-    output = (
-        residual + down[:, :width].astype(f32) + nn(rank_down, down_leave)
-    ).astype(bf16)[None]
+    down, rank_down = scatter_products([(hidden, w2, down_enter, True)], 3)
+    rank_down = rank_down.astype(bf16) * select_own_b
+    output = (residual + down + nn(rank_down, down_leave)).astype(bf16)[None]
 
     grad_down = out_grad[0]
     grad_all = gather_tokens(grad_down)
@@ -416,21 +634,12 @@
     d_hidden = nn(grad_all, w2) + nn(d_rank_down, down_enter)
     d_gate = (d_hidden * upper_val * sigma * (1.0 + gate_val * (1.0 - sigma))).astype(bf16)
     d_upper = (d_hidden * silu_gate).astype(bf16)
-    back = scatter_tokens(
-        jnp.concatenate(
-            [
-                nt(d_gate, w1) + nt(d_upper, w3),
-                nt(d_gate, gate_leave),
-                nt(d_upper, upper_leave),
-            ],
-            axis=1,
-        ).astype(bf16)
-    )
-    d_rank_gate = back[:, width : width + RANKS] * select_own_b
-    d_rank_upper = back[:, width + RANKS :] * select_own_b
-    d_normed_ffn = (
-        back[:, :width].astype(f32) + nn(d_rank_gate, gate_enter) + nn(d_rank_upper, upper_enter)
-    )
+    back, back_rank = scatter_products(
+        [(d_gate, w1, gate_leave, True), (d_upper, w3, upper_leave, True)], 4
+    )
+    d_rank_gate = (back_rank[:, :RANKS] * select_own).astype(bf16)
+    d_rank_upper = (back_rank[:, RANKS:] * select_own).astype(bf16)
+    d_normed_ffn = back + nn(d_rank_gate, gate_enter) + nn(d_rank_upper, upper_enter)
     d_residual = grad_down.astype(f32) + norm_backward(
         residual, inverse_ffn, ffn_gain, d_normed_ffn
     )
@@ -439,11 +648,9 @@
     d_rank_out = (nt(d_branch_all, out_leave) * select_all).astype(bf16)
     d_attn = (nt(d_branch_all, out_w) + nn(d_rank_out, out_enter)).astype(bf16)
     d_projected = attention_backward(slots, qs, kv, lse, d_attn, cosine, sine)
-    back_attn = scatter_tokens(
-        jnp.concatenate([nt(d_projected, qkv_w), nt(d_projected, qkv_leave)], axis=1).astype(bf16)
-    )
-    d_rank_qkv = back_attn[:, width:] * select_own_b
-    d_normed_attn = back_attn[:, :width].astype(f32) + nn(d_rank_qkv, qkv_enter)
+    back_attn, back_rank_qkv = scatter_products([(d_projected, qkv_w, qkv_leave, True)], 5)
+    d_rank_qkv = (back_rank_qkv * select_own).astype(bf16)
+    d_normed_attn = back_attn + nn(d_rank_qkv, qkv_enter)
     input_grad = (d_residual + norm_backward(inputs_f, inverse_attn, attn_gain, d_normed_attn))[
         None
     ]

time: 1280 us -> 859 us (0.67)
  waiting for transfers between devices: 781 us -> 121 us
  Pallas kernels: 36.5 us -> 429 us
  matrix products: 194 us -> 132 us
  blocking collectives: 117 us -> 73.4 us
  other arithmetic: 59 us -> 29 us
  local copies, waits for them, and re-layouts: 61 us -> 39.5 us
    pallas_call x0 -> x8, Pallas kernels: none -> 393 us  [the longest x4 218 us: scatter_products(): pl.pallas_call(functools.partial(scatter_kernel, modes), out_shape=(jax.S...]
    all_gather x4, waiting for transfers between devices: 241 us -> 34.9 us  [column_shard(): lax.all_gather(part, 'ad', axis=1, tiled=True).reshape(-1, columns // seq)]
    all_gather x4 -> x0, waiting for transfers between devices: 189 us -> none  [gather_tokens(): return lax.all_gather(x, 'seq', axis=0, tiled=True)]
    reduce_scatter x4 -> x0, waiting for transfers between devices: 185 us -> none  [scatter_tokens(): return lax.psum_scatter(x, 'seq', scatter_dimension=0, tiled=True)]
    dot_general x15 -> x6, matrix products: 92.5 us -> 31.4 us  [nt(): lax.dot_general(a, b, (((1,), (1,)), ((), ())), preferred_element_type=f32)]
    all_to_all x4 -> x2, blocking collectives: 80.8 us -> 36.9 us  [column_shard(): part = lax.all_to_all(w, 'seq', split_axis=1, concat_axis=0, tiled=True)]
    reduce_scatter x2, waiting for transfers between devices: 58.5 us -> 17.4 us  [reduced(): lax.psum_scatter(stack, 'seq', scatter_dimension=0, tiled=True)[0]]
    all_gather x1, waiting for transfers between devices: 33.5 us -> 0.01 us  [stack_ad(): return lax.all_gather(a, 'ad', axis=0, tiled=True)]
  transfers between devices with their start and end apart: 19 -> 13, of which waited for: 18 -> 6; matrix products, arithmetic and copies ran while one was open for 15% -> 15% of each run, Pallas kernels for 3% -> 31%
where the time goes in v2:
time: 859 us; the launch traced here: 850 us
  Pallas kernels  429 us (50%)
  matrix products  132 us (15%)
  waiting for transfers between devices  121 us (14%)
  blocking collectives  73.4 us (9%)
  local copies, waits for them, and re-layouts  39.5 us (5%)
  other arithmetic  29 us (3%)
  between operations  15.4 us (2%)
  starting transfers between devices  9.59 us (1%)
    pallas_call x4, Pallas kernels, scatter_products(): pl.pallas_call(functools.partial(scatter_kernel, modes), out_shape=(jax.S...  218 us
    pallas_call x4, Pallas kernels, gather_tokens(): pl.pallas_call(gather_kernel, out_shape=jax.ShapeDtypeStruct((PLANE * own...  174 us
    dot_general x14, matrix products, nn(): return jnp.dot(a, b, preferred_element_type=f32)  84.2 us
    reduce_scatter x2, waiting for transfers between devices, reduced(): mine = lax.psum_scatter(both, 'ad', scatter_dimension=0, tiled=True)  43.3 us
    all_to_all x2, blocking collectives, column_shard(): part = lax.all_to_all(w, 'seq', split_axis=1, concat_axis=0, tiled=True)  36.9 us
    all_gather x4, waiting for transfers between devices, column_shard(): lax.all_gather(part, 'ad', axis=1, tiled=True).reshape(-1, columns // seq)  34.9 us
    dot_general x6, matrix products, nt(): lax.dot_general(a, b, (((1,), (1,)), ((), ())), preferred_element_type=f32)  31.4 us
    all_gather x1, blocking collectives, stack_ad(): return lax.all_gather(a, 'ad', axis=0, tiled=True)  26.4 us
  transfers between devices with their start and end apart: 13, of which 6 were waited for; matrix products, arithmetic and copies ran while one was open for 15% of the time, Pallas kernels for 31%

profile of v2, /device:TPU:0, one launch (start us, length us, event | category | flops | bytes accessed | tf_op | source)
XLA Modules:
  0.0 849.9 jit_solution(17855824957561464523)
XLA Ops:
  9.2 5.2 all-to-all-start
  15.5 8.7 %all-to-all-done = bf16[64,8,512]{2,0,1:T(8,128)(2,1)S(1)} async-done(((bf16[64,8,512]{2,0,1:T(8,128)(2,1)}), bf16[64,8,512]{2,0,1:T(8,128)(2,1)S(1)}, u32[]{:S(2)}, u32[]{:S(2)}) %all-to-all-start) | async-done | bytes 524320 | tf_op jit(solution)/shard_map/all_to_all | solution.py:528
  31.8 18.4 %all_to_all.64 = bf16[64,8,1024]{2,0,1:T(8,128)(2,1)} all-to-all(bf16[64,8,1024]{2,0,1:T(8,128)(2,1)S(1)} %copy.49), channel_id=1, replica_groups=mesh['seq'=8,'ad'=4] {'seq'}, dimensions={1} | all-to-all | bytes 2097152 | tf_op jit(solution)/shard_map/all_to_all | solution.py:528
  51.5 18.4 %all_to_all.65 = bf16[64,8,1024]{2,0,1:T(8,128)(2,1)} all-to-all(bf16[64,8,1024]{2,0,1:T(8,128)(2,1)S(1)} %copy.48), channel_id=1, replica_groups=mesh['seq'=8,'ad'=4] {'seq'}, dimensions={1} | all-to-all | bytes 2097152 | tf_op jit(solution)/shard_map/all_to_all | solution.py:528
  82.7 26.4 %all_gather.34 = bf16[128,2560]{1,0:T(8,128)(2,1)S(1)} all-gather(bf16[32,2560]{1,0:T(8,128)(2,1)S(1)} %pad_maximum_fusion.3), channel_id=1, replica_groups=mesh['seq'=8,'ad'=4] {'ad'}, dimensions={0}, use_global_device_ids=true | all-gather | bytes 819200 | tf_op jit(solution)/shard_map/all_gather | solution.py:566
  109.1 44.2 %gather_tokens.4 = bf16[2048,2048]{1,0:T(8,128)(2,1)} custom-call(bf16[256,2048]{1,0:T(8,128)(2,1)} %fusion.14.own_ref), custom_call_target="tpu_custom_call" | custom-call | bytes 41943040 | tf_op jit(solution)/shard_map/gather_tokens/pallas_call | solution.py:362
  153.4 43.8 %gather_tokens.6 = bf16[2048,2048]{1,0:T(8,128)(2,1)} custom-call(bf16[256,2048]{1,0:T(8,128)(2,1)} %bitcast.154), custom_call_target="tpu_custom_call" | custom-call | bytes 41943040 | tf_op jit(solution)/shard_map/gather_tokens/pallas_call | solution.py:362
  202.2 5.8 fusion.9
  209.3 7.5 fusion.49
  219.7 15.3 %attention_forward.1 = (bf16[2048,256]{1,0:T(8,128)(2,1)}, bf16[4096,128]{1,0:T(8,128)(2,1)}, bf16[2048,256]{1,0:T(8,128)(2,1)}, f32[4096,1]{1,0:T(8,128)}) custom-call(s32[16]{0:T(128)} %get-tuple-element.23.slot_ref, f32[2048,512]{1,0:T(8,128)} %convolution_add_fusion.3.proj_ref, f32[1152,128]{1,0:T(8,128)} %get-tuple-element.74.cos_ref, ...), custom_call_target="tpu_custom_call" | custom-call | flops 4000000000 | bytes 10485760 | tf_op jit(solution)/shard_map/attention_forward/pallas_call | solution.py:172
  236.5 48.4 %scatter_products_2.1 = (f32[256,2048]{1,0:T(8,128)}, f32[256,128]{1,0:T(8,128)}) custom-call(bf16[2048,256]{1,0:T(8,128)(2,1)} %get-tuple-element.24.refs_0_, bf16[256,2048]{1,0:T(8,128)(2,1)} %all-gather.12.cloned.1.call-done.refs_1_, bf16[128,256]{1,0:T(8,128)(2,1)} %slice.118.refs_2_), custom_call_target="tpu_custom_call" | custom-call | flops 42281701376 | bytes 2097152 | tf_op jit(solution)/shard_map/scatter_products_2/pallas_call | solution.py:474
  292.1 43.5 %gather_tokens.5 = bf16[2048,2048]{1,0:T(8,128)(2,1)} custom-call(bf16[256,2048]{1,0:T(8,128)(2,1)} %multiply_convert_fusion.3.own_ref), custom_call_target="tpu_custom_call" | custom-call | bytes 41943040 | tf_op jit(solution)/shard_map/gather_tokens/pallas_call | solution.py:362
  335.6 6.9 fusion.8
  348.7 14.5 %fusion.51 = f32[2048,1024]{1,0:T(8,128)} fusion(bf16[2048,2048]{1,0:T(8,128)(2,1)} %gather_tokens.5, bf16[2048,1024]{1,0:T(8,128)(2,1)} %bitcast.190), kind=kOutput, calls=%fused_computation.145 | convolution fusion | flops 8589934592 | bytes 20971520 | tf_op jit(solution)/shard_map/dot_general | solution.py:34
  363.2 14.8 %fusion.50 = f32[2048,1024]{1,0:T(8,128)} fusion(bf16[2048,2048]{1,0:T(8,128)(2,1)} %gather_tokens.5, bf16[2048,1024]{1,0:T(8,128)(2,1)} %bitcast.192), kind=kOutput, calls=%fused_computation.144 | convolution fusion | flops 8589934592 | bytes 20971520 | tf_op jit(solution)/shard_map/dot_general | solution.py:34
  378.1 34.9 %all-gather.20.cloned.1.call-done = bf16[8,256,1024]{2,1,0:T(8,128)(2,1)} async-done(((bf16[8,64,1024]{2,1,0:T(8,128)(2,1)}), bf16[8,256,1024]{2,1,0:T(8,128)(2,1)}) %all-gather.20.cloned.1.call-update) | async-done | bytes 4194320 | tf_op jit(solution)/shard_map/all_gather | solution.py:530
  412.9 14.5 %fusion.52 = f32[2048,1024]{1,0:T(8,128)} fusion(bf16[2048,2048]{1,0:T(8,128)(2,1)} %gather_tokens.6, bf16[2048,1024]{1,0:T(8,128)(2,1)} %bitcast.194), kind=kOutput, calls=%fused_computation.146 | convolution fusion | flops 8589934592 | bytes 20971520 | tf_op jit(solution)/shard_map/dot_general | solution.py:34
  430.9 4.6 convolution_add_fusion.2
  435.5 11.1 %multiply_convert_fusion = (bf16[2048,1024]{1,0:T(8,128)(2,1)}, bf16[2048,1024]{1,0:T(8,128)(2,1)}, bf16[2048,1024]{1,0:T(8,128)(2,1)}) fusion(f32[2048,1024]{1,0:T(8,128)} %convolution_add_fusion.2, f32[2048,1024]{1,0:T(8,128)S(1)} %convolution_add_fusion.1, f32[2048,1024]{1,0:T(8,128)} %fusion.52, bf16[2048,128]{1,0:T(8,128)(2,1)S(1)} %copy-done.20, ...), kind=kOutput, calls=%fused_computation | convolution fusion | flops 570425344 | bytes 38535168 | tf_op jit(solution)/shard_map/dot_general | solution.py:34
  446.6 65.9 %scatter_products_4.1 = (f32[256,2048]{1,0:T(8,128)}, f32[256,256]{1,0:T(8,128)}) custom-call(bf16[2048,1024]{1,0:T(8,128)(2,1)} %get-tuple-element.39.refs_0_, bf16[2048,1024]{1,0:T(8,128)(2,1)} %get-tuple-element.38.refs_1_, bf16[2048,1024]{1,0:T(8,128)(2,1)} %bitcast.193, bf16[2048,1024]{1,0:T(8,128)(2,1)} %bitcast.191, ...), custom_call_target="tpu_custom_call" | custom-call | flops 59327352832 | bytes 16777216 | tf_op jit(solution)/shard_map/scatter_products_4/pallas_call | solution.py:474
  523.4 42.7 %gather_tokens.7 = bf16[2048,2048]{1,0:T(8,128)(2,1)} custom-call(bf16[256,2048]{1,0:T(8,128)(2,1)} %copy-done.8), custom_call_target="tpu_custom_call" | custom-call | bytes 41943040 | tf_op jit(solution)/shard_map/gather_tokens/pallas_call | solution.py:362
  571.8 53.7 %scatter_products_3.1 = (f32[256,2048]{1,0:T(8,128)}, f32[256,128]{1,0:T(8,128)}) custom-call(bf16[2048,1024]{1,0:T(8,128)(2,1)} %get-tuple-element.40.refs_0_, bf16[2048,1024]{1,0:T(8,128)(2,1)} %bitcast.195, bf16[128,1024]{1,0:T(8,128)(2,1)} %get-tuple-element.45.refs_2_), custom_call_target="tpu_custom_call" | custom-call | flops 49126805504 | bytes 8388608 | tf_op jit(solution)/shard_map/scatter_products_3/pallas_call | solution.py:474
  629.0 6.0 fusion.7
  635.0 6.5 fusion.53
  643.8 21.4 %attention_backward.1.refs_0_ = bf16[2048,512]{1,0:T(8,128)(2,1)} custom-call(s32[16]{0:T(128)} %get-tuple-element.23.slot_ref, bf16[4096,128]{1,0:T(8,128)(2,1)} %get-tuple-element.31.qs_ref, bf16[2048,256]{1,0:T(8,128)(2,1)} %get-tuple-element.32.kv_ref, f32[4096,1]{1,0:T(8,128)} %get-tuple-element.33.lse_ref, bf16[2048,256]{1,0:T(8,128)(2,1)} %fusion.4.grad_ref, ...), custom_call_target="tpu_custom_call" | custom-call | flops 8999999488 | bytes 10485760 | tf_op jit(solution)/shard_map/attention_backward/pallas_call | solution.py:253
  665.1 50.4 %scatter_products_5.1 = (f32[256,2048]{1,0:T(8,128)}, f32[256,128]{1,0:T(8,128)}) custom-call(bf16[2048,512]{1,0:T(8,128)(2,1)} %attention_backward.1.refs_0_, bf16[2048,512]{1,0:T(8,128)(2,1)} %bitcast.197, bf16[128,512]{1,0:T(8,128)(2,1)} %slice.117.refs_2_), custom_call_target="tpu_custom_call" | custom-call | flops 44563402752 | bytes 4194304 | tf_op jit(solution)/shard_map/scatter_products_5/pallas_call | solution.py:474
  722.1 3.7 fusion.22
  732.1 17.3 %reduce-scatter.5.cloned.1.call-done = bf16[1,128,256]{2,1,0:T(8,128)(2,1)} async-done(((bf16[8,128,256]{2,1,0:T(8,128)(2,1)}), bf16[1,128,256]{2,1,0:T(8,128)(2,1)}) %reduce-scatter.5.cloned.1.call-update) | async-done | bytes 65552 | tf_op jit(solution)/shard_map/reduce_scatter | solution.py:665
  751.0 29.7 %reduce-scatter.11.cloned.1.call-done = bf16[32,4352]{1,0:T(8,128)(2,1)} async-done(((bf16[128,4352]{1,0:T(8,128)(2,1)}), bf16[32,4352]{1,0:T(8,128)(2,1)}) %reduce-scatter.11.cloned.1.call-update) | async-done | bytes 278544 | tf_op jit(solution)/shard_map/reduce_scatter | solution.py:668
  787.9 13.6 %reduce-scatter.7.cloned.1.call-done = bf16[32,768]{1,0:T(8,128)(2,1)} async-done(((bf16[128,768]{1,0:T(8,128)(2,1)}), bf16[32,768]{1,0:T(8,128)(2,1)}) %reduce-scatter.7.cloned.1.call-update) | async-done | bytes 49168 | tf_op jit(solution)/shard_map/reduce_scatter | solution.py:668
  801.5 10.1 %all-gather = bf16[256,768]{1,0:T(8,128)(2,1)S(1)} all-gather(bf16[32,768]{1,0:T(8,128)(2,1)} %reduce-scatter.7.cloned.1.call-done), channel_id=2, replica_groups=mesh['seq'=8,'ad'=4] {'seq'}, dimensions={0}, use_global_device_ids=true | all-gather | bytes 442368 | tf_op jit(solution)/shard_map/all_gather | solution.py:669
  813.8 16.2 %all-gather.22.cloned.1.call-done = bf16[256,4352]{1,0:T(8,128)(2,1)} async-done(((bf16[32,4352]{1,0:T(8,128)(2,1)}), bf16[256,4352]{1,0:T(8,128)(2,1)}) %all-gather.22.cloned.1.call-update) | async-done | bytes 2228240 | tf_op jit(solution)/shard_map/all_gather | solution.py:669
  (248 shorter events, 110.2 us)
Async XLA Ops:
  7.2 68.7 %copy-start = (bf16[2,16,4096]{2,1,0:T(8,128)(2,1)S(1)}, bf16[2,16,4096]{2,1,0:T(8,128)(2,1)}, u32[]{:S(2)}) copy-start(bf16[2,16,4096]{2,1,0:T(8,128)(2,1)} %param.27) | copy-start | bytes 786436
  7.2 17.8 %copy-start.40 = (bf16[2,16,2048]{2,1,0:T(8,128)(2,1)S(1)}, bf16[2,16,2048]{2,1,0:T(8,128)(2,1)}, u32[]{:S(2)}) copy-start(bf16[2,16,2048]{2,1,0:T(8,128)(2,1)} %param.29) | copy-start | bytes 393220
  7.2 17.9 %copy-start.41 = (bf16[2,16,2048]{2,1,0:T(8,128)(2,1)S(1)}, bf16[2,16,2048]{2,1,0:T(8,128)(2,1)}, u32[]{:S(2)}) copy-start(bf16[2,16,2048]{2,1,0:T(8,128)(2,1)} %param.33) | copy-start | bytes 393220
  7.2 18.6 %copy-start.33 = (bf16[2,2,16,8192]{3,2,1,0:T(8,128)(2,1)S(1)}, bf16[2,2,16,8192]{3,2,1,0:T(8,128)(2,1)}, u32[]{:S(2)}) copy-start(bf16[2,2,16,8192]{3,2,1,0:T(8,128)(2,1)} %param.31) | copy-start | bytes 3145732
  9.2 14.9 %all-to-all-start = ((bf16[64,8,512]{2,0,1:T(8,128)(2,1)}), bf16[64,8,512]{2,0,1:T(8,128)(2,1)S(1)}, u32[]{:S(2)}, u32[]{:S(2)}) async-start(bf16[64,8,512]{2,0,1:T(8,128)(2,1)} %bitcast.152), calls=%async_computation | async-start | bytes 1048576 | tf_op jit(solution)/shard_map/all_to_all | solution.py:528
  14.4 194.9 %all-gather.10.cloned.1.call-start = ((), (), s32[]{:S(2)}) async-start(), calls=%async_computation.8 | async-start | bytes 2621440 | tf_op jit(solution)/shard_map/all_gather | solution.py:530
  24.9 210.1 %all-gather.14.cloned.1.call-start = ((), (), s32[]{:S(2)}) async-start(), calls=%async_computation.10 | async-start | bytes 3686400 | tf_op jit(solution)/shard_map/all_gather | solution.py:566
  27.7 208.8 %all-gather.12.cloned.1.call-start = ((), (), s32[]{:S(2)}) async-start(), calls=%async_computation.9 | async-start | bytes 1310720 | tf_op jit(solution)/shard_map/all_gather | solution.py:602
  28.4 320.3 %all-gather.18.cloned.1.call-start = ((), (), s32[]{:S(2)}) async-start(), calls=%async_computation.12 | async-start | bytes 5242880 | tf_op jit(solution)/shard_map/all_gather | solution.py:530
  50.3 313.0 %all-gather.16.cloned.1.call-start = ((), (), s32[]{:S(2)}) async-start(), calls=%async_computation.11 | async-start | bytes 5242880 | tf_op jit(solution)/shard_map/all_gather | solution.py:530
  70.6 7.6 copy-start.47
  72.2 135.8 %all-to-all-start.3 = ((bf16[64,8,1024]{2,0,1:T(8,128)(2,1)}), bf16[64,8,1024]{2,0,1:T(8,128)(2,1)S(1)}, u32[]{:S(2)}, u32[]{:S(2)}) async-start(bf16[64,8,1024]{2,0,1:T(8,128)(2,1)} %copy.50), calls=%async_computation.3 | async-start | bytes 2097152 | tf_op jit(solution)/shard_map/all_to_all | solution.py:528
  75.7 337.2 %all-gather.20.cloned.1.call-start = ((), (), s32[]{:S(2)}) async-start(), calls=%async_computation.13 | async-start | bytes 5242880 | tf_op jit(solution)/shard_map/all_gather | solution.py:530
  75.8 269.8 %copy-start.55 = (s32[128]{0:T(128)}, s32[128]{0:T(128)S(1)}, u32[]{:S(2)}) copy-start(s32[128]{0:T(128)S(1)} %and_select_fusion) | copy-start | bytes 1540
  76.9 32.3 %copy-start.49 = (f32[256]{0:T(256)}, f32[256]{0:T(256)S(1)}, u32[]{:S(2)}) copy-start(f32[256]{0:T(256)S(1)} %get-tuple-element.62) | copy-start | bytes 3076
  76.9 268.6 %copy-start.43 = (s32[2048]{0:T(1024)}, s32[2048]{0:T(1024)S(1)}, u32[]{:S(2)}) copy-start(s32[2048]{0:T(1024)S(1)} %broadcast_bitcast_fusion) | copy-start | bytes 24580
  109.1 107.8 %copy-start.18 = (bf16[128,2560]{1,0:T(8,128)(2,1)}, bf16[128,2560]{1,0:T(8,128)(2,1)S(1)}, u32[]{:S(2)}) copy-start(bf16[128,2560]{1,0:T(8,128)(2,1)S(1)} %all_gather.34) | copy-start | bytes 1966084
  208.0 8.9 %copy-start.28 = (bf16[2048,128]{1,0:T(8,128)(2,1)}, bf16[2048,128]{1,0:T(8,128)(2,1)S(1)}, u32[]{:S(2)}) copy-start(bf16[2048,128]{1,0:T(8,128)(2,1)S(1)} %fusion.9) | copy-start | bytes 1572868
  209.1 508.8 %reduce-scatter.9.cloned.1.call-start = ((), (), s32[]{:S(2)}) async-start(), calls=%async_computation.16 | async-start | bytes 2359296 | tf_op jit(solution)/shard_map/reduce_scatter | solution.py:665
  288.9 46.7 %copy-start.51 = (f32[256]{0:T(256)}, f32[256]{0:T(256)S(1)}, u32[]{:S(2)}) copy-start(f32[256]{0:T(256)S(1)} %get-tuple-element.64) | copy-start | bytes 3076
  335.6 6.9 copy-start.11
  412.9 14.5 %copy-start.12 = (f32[2048,1024]{1,0:T(8,128)S(1)}, f32[2048,1024]{1,0:T(8,128)}, u32[]{:S(2)}) copy-start(f32[2048,1024]{1,0:T(8,128)} %fusion.51) | copy-start | bytes 25165828
  412.9 14.5 %copy-start.22 = (bf16[2048,128]{1,0:T(8,128)(2,1)S(1)}, bf16[2048,128]{1,0:T(8,128)(2,1)}, u32[]{:S(2)}) copy-start(bf16[2048,128]{1,0:T(8,128)(2,1)} %fusion.11) | copy-start | bytes 1572868
  446.6 67.1 %copy-start.6 = (bf16[256,2048]{1,0:T(8,128)(2,1)S(1)}, bf16[256,2048]{1,0:T(8,128)(2,1)}, u32[]{:S(2)}) copy-start(bf16[256,2048]{1,0:T(8,128)(2,1)} %multiply_convert_fusion.3.own_ref) | copy-start | bytes 3145732
  628.7 120.7 %reduce-scatter.5.cloned.1.call-start = ((), (), s32[]{:S(2)}) async-start(), calls=%async_computation.14 | async-start | bytes 589824 | tf_op jit(solution)/shard_map/reduce_scatter | solution.py:665
  635.0 6.5 copy-start.26
  665.1 51.4 %copy-start.9 = (bf16[256,2048]{1,0:T(8,128)(2,1)S(1)}, bf16[256,2048]{1,0:T(8,128)(2,1)}, u32[]{:S(2)}) copy-start(bf16[256,2048]{1,0:T(8,128)(2,1)} %fusion.14.own_ref) | copy-start | bytes 3145732
  717.8 62.9 %reduce-scatter.11.cloned.1.call-start = ((), (), s32[]{:S(2)}) async-start(), calls=%async_computation.17 | async-start | bytes 1392640 | tf_op jit(solution)/shard_map/reduce_scatter | solution.py:668
  729.7 51.0 %copy-start.5 = (bf16[1,256,2048]{2,1,0:T(8,128)(2,1)S(1)}, bf16[1,256,2048]{2,1,0:T(8,128)(2,1)}, u32[]{:S(2)}) copy-start(bf16[1,256,2048]{2,1,0:T(8,128)(2,1)} %param.17) | copy-start | bytes 3145732
  729.7 51.0 %copy-start.48 = (f32[2048]{0:T(1024)S(1)}, f32[2048]{0:T(1024)}, u32[]{:S(2)}) copy-start(f32[2048]{0:T(1024)} %param.21) | copy-start | bytes 24580
  729.7 71.8 %reduce-scatter.7.cloned.1.call-start = ((), (), s32[]{:S(2)}) async-start(), calls=%async_computation.15 | async-start | bytes 245760 | tf_op jit(solution)/shard_map/reduce_scatter | solution.py:668
  751.0 79.0 %all-gather.22.cloned.1.call-start = ((), (), s32[]{:S(2)}) async-start(), calls=%async_computation.18 | async-start | bytes 2506752 | tf_op jit(solution)/shard_map/all_gather | solution.py:669
  (41 other events, 131.2 us)
Sparse Core Ops, SparseCore 0:
  25.1 45.0 all-gather.9
  72.3 69.3 all-gather.13
  143.3 26.6 all-gather.11
  171.4 80.1 all-gather.17
  253.0 79.2 all-gather.15
  333.6 79.2 all-gather.19
  628.8 38.6 reduce-scatter.8
  717.9 31.4 reduce-scatter.4
  752.3 28.3 reduce-scatter.10
  783.4 18.1 reduce-scatter.6
  803.4 26.5 all-gather.21

commit v3 on v2

--- a/solution.py
+++ b/solution.py
@@ -7,6 +7,7 @@
 from jax.experimental import pallas as pl
 from jax.experimental.pallas import tpu as pltpu
 from jax.sharding import PartitionSpec as P
+
 
 QUERY_HEADS = 16
 KEY_VALUE_HEADS = 8
@@ -19,7 +20,6 @@
 CONTS = 8
 BLOCK = 128
 SLOTS = 16
-GTOK = SLOTS * BLOCK
 RANKS = NA * R
 
 eps_norm = 1e-05
@@ -316,74 +316,100 @@
             copy.wait_send()
 
 
-def gather_kernel(own_ref, all_ref, send_sem, recv_sem):
-    own = own_ref.shape[0]
+def gather_kernel(count, *refs):
+    own_refs, all_refs = refs[:count], refs[count : 2 * count]
+    send_sem, recv_sem = refs[2 * count :]
+    own = own_refs[0].shape[0]
     half = own // 2
     me, p, nx, ny, nd = neighbours()
     greet(p, nx, ny)
     links = Links(send_sem, recv_sem)
-
-    def piece(i, h):
-        return all_ref.at[pl.ds(pl.multiple_of(i * own + h * half, half), half), :]
-
-    mine = own_ref.at
-    links.start(0, mine[:half, :], piece(me, 0), nx)
-    links.start(1, mine[half:, :], piece(me, 1), ny)
-    links.start(2, mine[half:, :], piece(me, 1), nx)
-    links.start(3, mine[:half, :], piece(me, 0), ny)
-    block = all_ref.at[pl.ds(pl.multiple_of(me * own, own), own), :]
-    links.start(4, own_ref, block, p)
-    all_ref[pl.ds(pl.multiple_of(me * own, own), own), :] = own_ref[...]
-
-    links.arrived(0)
-    links.start(5, piece(nx, 0), piece(nx, 0), ny)
-    links.start(7, piece(nx, 0), piece(nx, 0), p)
-    links.arrived(1)
-    links.start(6, piece(ny, 1), piece(ny, 1), nx)
-    links.start(8, piece(ny, 1), piece(ny, 1), p)
-    links.arrived(2)
-    links.start(9, piece(nx, 1), piece(nx, 1), p)
-    links.arrived(3)
-    links.start(10, piece(ny, 0), piece(ny, 0), p)
-    links.arrived(5)
-    links.start(11, piece(nd, 0), piece(nd, 0), p)
-    links.arrived(6)
-    links.start(12, piece(nd, 1), piece(nd, 1), p)
+    arrays = range(count)
+
+    def piece(j, i, h):
+        return all_refs[j].at[pl.ds(pl.multiple_of(i * own + h * half, half), half), :]
+
+    def mine(j, h):
+        return own_refs[j].at[h * half : (h + 1) * half, :]
+
+    def block(j):
+        return all_refs[j].at[pl.ds(pl.multiple_of(me * own, own), own), :]
+
+    def each(k, copy):
+        for j in arrays:
+            links.start(13 * j + k, *copy(j))
+
+    def arrived(k):
+        for j in arrays:
+            links.arrived(13 * j + k)
+
+    each(0, lambda j: (mine(j, 0), piece(j, me, 0), nx))
+    each(1, lambda j: (mine(j, 1), piece(j, me, 1), ny))
+    each(2, lambda j: (mine(j, 1), piece(j, me, 1), nx))
+    each(3, lambda j: (mine(j, 0), piece(j, me, 0), ny))
+    each(4, lambda j: (own_refs[j], block(j), p))
+    for j in arrays:
+        all_refs[j][pl.ds(pl.multiple_of(me * own, own), own), :] = own_refs[j][...]
+
+    def pass_on(k, i, h, to):
+        each(k, lambda j: (piece(j, i, h), piece(j, i, h), to))
+
+    arrived(0)
+    pass_on(5, nx, 0, ny)
+    pass_on(7, nx, 0, p)
+    arrived(1)
+    pass_on(6, ny, 1, nx)
+    pass_on(8, ny, 1, p)
+    arrived(2)
+    pass_on(9, nx, 1, p)
+    arrived(3)
+    pass_on(10, ny, 0, p)
+    arrived(5)
+    pass_on(11, nd, 0, p)
+    arrived(6)
+    pass_on(12, nd, 1, p)
     for k in (4, 7, 8, 9, 10, 11, 12):
-        links.arrived(k)
+        arrived(k)
     links.drain()
 
 
-def gather_tokens(x):
+def gather_tokens(collective_id, *arrays):
     if lax.axis_size("seq") != PLANE:
-        return lax.all_gather(x, "seq", axis=0, tiled=True)
-    own, width = x.shape
+        return tuple(lax.all_gather(x, "seq", axis=0, tiled=True) for x in arrays)
     vm = pl.BlockSpec(memory_space=pltpu.VMEM)
+    count = len(arrays)
+    size = sum(x.shape[0] * x.shape[1] for x in arrays)
     return pl.pallas_call(
-        gather_kernel,
-        out_shape=jax.ShapeDtypeStruct((PLANE * own, width), x.dtype),
-        in_specs=[vm],
-        out_specs=vm,
-        scratch_shapes=[pltpu.SemaphoreType.DMA((13,)), pltpu.SemaphoreType.DMA((13,))],
-        compiler_params=pltpu.CompilerParams(collective_id=1, has_side_effects=True),
+        functools.partial(gather_kernel, count),
+        out_shape=tuple(
+            jax.ShapeDtypeStruct((PLANE * x.shape[0], x.shape[1]), x.dtype) for x in arrays
+        ),
+        in_specs=[vm] * count,
+        out_specs=(vm,) * count,
+        scratch_shapes=[
+            pltpu.SemaphoreType.DMA((13 * count,)),
+            pltpu.SemaphoreType.DMA((13 * count,)),
+        ],
+        compiler_params=pltpu.CompilerParams(collective_id=collective_id, has_side_effects=True),
         cost_estimate=pl.CostEstimate(
-            flops=0, bytes_accessed=10 * PLANE * own * width, transcendentals=0
+            flops=0, bytes_accessed=10 * PLANE * size, transcendentals=0
         ),
-        name="gather_tokens",
-    )(x)
+    )(*arrays)
 
 
 COLS = 256
 
 
-def scatter_kernel(modes, *refs):
-    n = len(modes)
-    a_refs, b_refs, r_refs = refs[:n], refs[n : 2 * n], refs[2 * n : 3 * n]
-    out_ref, rank_ref, theirs, cores, sums, relay, last, send_sem, recv_sem = refs[3 * n :]
+def scatter_kernel(modes, rank_from, count, *refs):
+    n, m = len(modes), len(rank_from)
+    a_refs, b_refs, r_refs = refs[:count], refs[count : count + n], refs[count + n : count + n + m]
+    refs = refs[count + n + m :]
+    out_ref, rank_ref = (refs[0], refs[1]) if m else (refs[0], None)
+    theirs, cores, sums, relay, last, send_sem, recv_sem = refs[2 if m else 1 :]
     own, width = out_ref.shape
-    ranks = rank_ref.shape[1]
     half = own // 2
-    per = ranks // n
+    per = RANKS
+    ranks = m * per
     me, p, nx, ny, nd = neighbours()
     greet(p, nx, ny)
     links = Links(send_sem, recv_sem)
@@ -401,8 +427,9 @@
             return 0
 
         lax.fori_loop(0, width // COLS, tile, 0)
-        for j, (a, r) in enumerate(zip(a_refs, r_refs)):
-            store(slice(width + j * per, width + (j + 1) * per), nt(a[rows, :], r[...]))
+        for j, r in enumerate(r_refs):
+            product = nt(a_refs[rank_from[j]][rows, :], r[...])
+            store(slice(width + j * per, width + (j + 1) * per), product)
 
     def for_partner(slot, i):
         def store(cols, value):
@@ -451,34 +478,34 @@
         links.arrived(k)
     both = lambda cols: last[0, :, cols].astype(f32) + last[1, :, cols].astype(f32)
     out_ref[...] = out_ref[...] + both(slice(0, width))
-    rank_ref[...] = rank_ref[...] + both(slice(width, width + ranks))
+    if m:
+        rank_ref[...] = rank_ref[...] + both(slice(width, width + ranks))
     links.drain()
 
 
-def scatter_products(terms, collective_id):
-    modes = tuple(t[3] for t in terms)
-    a, b, r = ([t[k] for t in terms] for k in range(3))
+def scatter_products(a, b, modes, rank_maps, rank_from, collective_id):
     width = b[0].shape[0] if modes[0] else b[0].shape[1]
-    ranks = sum(x.shape[0] for x in r)
+    ranks = RANKS * len(rank_maps)
     seq = lax.axis_size("seq")
     rows = a[0].shape[0]
     own = rows // seq
     if seq != PLANE:
         total = sum(nt(x, y) if m else nn(x, y) for x, y, m in zip(a, b, modes))
-        both = jnp.concatenate([total] + [nt(x, y) for x, y in zip(a, r)], axis=1).astype(bf16)
+        extra = [nt(a[i], y) for i, y in zip(rank_from, rank_maps)]
+        both = jnp.concatenate([total] + extra, axis=1).astype(bf16)
         both = lax.psum_scatter(both, "seq", scatter_dimension=0, tiled=True).astype(f32)
         return both[:, :width], both[:, width:]
     vm = pl.BlockSpec(memory_space=pltpu.VMEM)
     whole = width + ranks
     depth = sum(x.shape[1] for x in a)
-    return pl.pallas_call(
-        functools.partial(scatter_kernel, modes),
-        out_shape=(
-            jax.ShapeDtypeStruct((own, width), f32),
-            jax.ShapeDtypeStruct((own, ranks), f32),
-        ),
-        in_specs=[vm] * (3 * len(terms)),
-        out_specs=(vm, vm),
+    shapes = [jax.ShapeDtypeStruct((own, width), f32)]
+    if ranks:
+        shapes.append(jax.ShapeDtypeStruct((own, ranks), f32))
+    out = pl.pallas_call(
+        functools.partial(scatter_kernel, tuple(modes), tuple(rank_from), len(a)),
+        out_shape=tuple(shapes),
+        in_specs=[vm] * (len(a) + len(b) + len(rank_maps)),
+        out_specs=(vm,) * len(shapes),
         scratch_shapes=[
             pltpu.VMEM((4, own, whole), bf16),
             pltpu.VMEM((4, own, whole), bf16),
@@ -494,8 +521,8 @@
             bytes_accessed=rows * depth * 4,
             transcendentals=0,
         ),
-        name=f"scatter_products_{collective_id}",
-    )(*a, *b, *r)
+    )(*a, *b, *rank_maps)
+    return (out[0], out[1]) if ranks else (out[0], None)
 
 
 def head_columns(w, seq):
@@ -522,12 +549,61 @@
     return jnp.concatenate([q, jnp.sum(g[..., own:, :], axis=-3)], axis=-2).reshape(*lead, -1)
 
 
-def column_shard(w):
+def exchange_kernel(count, *refs):
+    in_refs, out_refs = refs[:count], refs[count : 2 * count]
+    send_sem, recv_sem = refs[2 * count :]
+    me = lax.axis_index("seq")
+    others = [lax.rem(me + k, PLANE) for k in range(1, PLANE)]
+    greet(*others)
+    links = Links(send_sem, recv_sem)
+
+    def columns(j, i):
+        part = in_refs[j].shape[1] // PLANE
+        return pl.ds(pl.multiple_of(i * part, part), part)
+
+    for j in range(count):
+        for k, other in enumerate(others):
+            links.start(
+                (PLANE - 1) * j + k, in_refs[j].at[:, columns(j, other)], out_refs[j].at[me], other
+            )
+    for j in range(count):
+        out_refs[j][me] = in_refs[j][:, columns(j, me)]
+    for k in range((PLANE - 1) * count):
+        links.arrived(k)
+    links.drain()
+
+
+def exchange_columns(collective_id, *arrays):
     seq = lax.axis_size("seq")
-    rows, columns = w.shape
-    part = lax.all_to_all(w, "seq", split_axis=1, concat_axis=0, tiled=True)
-    part = part.reshape(seq, rows, columns // seq)
-    return lax.all_gather(part, "ad", axis=1, tiled=True).reshape(-1, columns // seq)
+    shapes = tuple(
+        jax.ShapeDtypeStruct((seq, w.shape[0], w.shape[1] // seq), w.dtype) for w in arrays
+    )
+    if seq != PLANE:
+        return tuple(
+            lax.all_to_all(w, "seq", split_axis=1, concat_axis=0, tiled=True).reshape(t.shape)
+            for w, t in zip(arrays, shapes)
+        )
+    vm = pl.BlockSpec(memory_space=pltpu.VMEM)
+    count = len(arrays)
+    copies = (PLANE - 1) * count
+    return pl.pallas_call(
+        functools.partial(exchange_kernel, count),
+        out_shape=shapes,
+        in_specs=[vm] * count,
+        out_specs=(vm,) * count,
+        scratch_shapes=[
+            pltpu.SemaphoreType.DMA((copies,)),
+            pltpu.SemaphoreType.DMA((copies,)),
+        ],
+        compiler_params=pltpu.CompilerParams(collective_id=collective_id, has_side_effects=True),
+        cost_estimate=pl.CostEstimate(
+            flops=0, bytes_accessed=20 * sum(w.size for w in arrays), transcendentals=0
+        ),
+    )(*arrays)
+
+
+def all_rows(part):
+    return lax.all_gather(part, "ad", axis=1, tiled=True).reshape(-1, part.shape[2])
 
 
 def local(
@@ -574,49 +650,50 @@
     cosine, sine = rope_tables()
 
     flat = lambda a: a.reshape(-1, a.shape[-1])
-    first = stack_ad(jnp.concatenate([flat(qkv_a), my_columns(head_columns(flat(qkv_b), seq), qkv_part)], axis=1))
-    qkv_enter, qkv_leave = first[:, :width], first[:, width:]
-    second = stack_ad(
-        jnp.concatenate(
-            [
-                flat(out_b),
-                flat(ffn_in_a[:, 0]),
-                flat(ffn_in_a[:, 1]),
-                flat(ffn_out_b),
-                my_columns(flat(out_a), head_part),
-                my_columns(flat(ffn_in_b[:, 0]), ff_part),
-                my_columns(flat(ffn_in_b[:, 1]), ff_part),
-                my_columns(flat(ffn_out_a), ff_part),
-            ],
-            axis=1,
-        )
-    )
-    cuts = [width] * 4 + [head_part] + [ff_part] * 3
-    pieces, at = [], 0
-    for c in cuts:
-        pieces.append(second[:, at : at + c])
+    whole_maps = [qkv_a, out_b, ffn_in_a[:, 0], ffn_in_a[:, 1], ffn_out_b]
+    part_maps = [
+        (head_columns(flat(qkv_b), seq), qkv_part),
+        (flat(out_a), head_part),
+        (flat(ffn_in_b[:, 0]), ff_part),
+        (flat(ffn_in_b[:, 1]), ff_part),
+        (flat(ffn_out_a), ff_part),
+    ]
+    wpart = width // seq
+    pieces = [my_columns(flat(m), wpart) for m in whole_maps]
+    pieces += [my_columns(m, part) for m, part in part_maps]
+    pieces.append(wo.reshape(pieces[0].shape[0], -1))
+    (qkv_cols,) = exchange_columns(10, wqkv)
+    qkv_w = all_rows(qkv_cols)
+    together = stack_ad(jnp.concatenate(pieces, axis=1))
+    at = len(whole_maps) * wpart
+    (spread,) = gather_tokens(7, together[:, :at])
+    spread = spread.reshape(seq, RANKS, len(whole_maps), wpart).transpose(2, 1, 0, 3)
+    spread = spread.reshape(len(whole_maps), RANKS, width)
+    qkv_enter, out_leave, gate_enter, upper_enter, down_leave = (
+        spread[k] for k in range(len(whole_maps))
+    )
+    parts = []
+    for _, c in part_maps:
+        parts.append(together[:, at : at + c])
         at += c
-    out_leave, gate_enter, upper_enter, down_leave, out_enter, gate_leave, upper_leave, down_enter = pieces
-
-    qkv_w = column_shard(wqkv)
-    out_w = lax.all_gather(wo, "ad", axis=0, tiled=True)
-    w1 = column_shard(ffn[:, 0])
-    w3 = column_shard(ffn[:, 1])
-    w2 = column_shard(ffn[:, 2])
+    qkv_leave, out_enter, gate_leave, upper_leave, down_enter = parts
+    out_w = together[:, at:].reshape(-1, width)
+
+    w1, w3, w2 = map(all_rows, exchange_columns(11, ffn[:, 0], ffn[:, 1], ffn[:, 2]))
 
     inputs_f = tokens[0].astype(f32)
     normed, inverse_attn = norm_forward(inputs_f, attn_gain)
     normed_attn = normed.astype(bf16)
-    normed_attn_all = gather_tokens(normed_attn)
+    (normed_attn_all,) = gather_tokens(1, normed_attn)
     rank_qkv = nt(normed_attn_all, qkv_enter).astype(bf16) * select_all_b
     projected = nn(normed_attn_all, qkv_w) + nn(rank_qkv, qkv_leave)
     attn, qs, kv, lse = attention_forward(slots, projected, cosine, sine)
-    branch, rank_out = scatter_products([(attn, out_w, out_enter, False)], 2)
+    branch, rank_out = scatter_products([attn], [out_w], [False], [out_enter], [0], 2)
     rank_out = rank_out.astype(bf16) * select_own_b
     residual = inputs_f + branch + nn(rank_out, out_leave)
     normed_two, inverse_ffn = norm_forward(residual, ffn_gain)
     normed_ffn = normed_two.astype(bf16)
-    normed_ffn_all = gather_tokens(normed_ffn)
+    (normed_ffn_all,) = gather_tokens(1, normed_ffn)
     rank_gate = nt(normed_ffn_all, gate_enter).astype(bf16) * select_all_b
     rank_upper = nt(normed_ffn_all, upper_enter).astype(bf16) * select_all_b
     gate_val = nn(normed_ffn_all, w1) + nn(rank_gate, gate_leave)
@@ -624,49 +701,47 @@
     sigma = jax.nn.sigmoid(gate_val)
     silu_gate = gate_val * sigma
     hidden = (silu_gate * upper_val).astype(bf16)
-    down, rank_down = scatter_products([(hidden, w2, down_enter, True)], 3)
-    rank_down = rank_down.astype(bf16) * select_own_b
-    output = (residual + down + nn(rank_down, down_leave)).astype(bf16)[None]
-
     grad_down = out_grad[0]
-    grad_all = gather_tokens(grad_down)
+    (grad_all,) = gather_tokens(1, grad_down)
     d_rank_down = (nt(grad_all, down_leave) * select_all).astype(bf16)
     d_hidden = nn(grad_all, w2) + nn(d_rank_down, down_enter)
     d_gate = (d_hidden * upper_val * sigma * (1.0 + gate_val * (1.0 - sigma))).astype(bf16)
     d_upper = (d_hidden * silu_gate).astype(bf16)
     back, back_rank = scatter_products(
-        [(d_gate, w1, gate_leave, True), (d_upper, w3, upper_leave, True)], 4
+        [d_gate, d_upper, hidden],
+        [w1, w3],
+        [True, True],
+        [gate_leave, upper_leave, down_enter],
+        [0, 1, 2],
+        4,
     )
     d_rank_gate = (back_rank[:, :RANKS] * select_own).astype(bf16)
-    d_rank_upper = (back_rank[:, RANKS:] * select_own).astype(bf16)
+    d_rank_upper = (back_rank[:, RANKS : 2 * RANKS] * select_own).astype(bf16)
+    rank_down = back_rank[:, 2 * RANKS :].astype(bf16) * select_own_b
     d_normed_ffn = back + nn(d_rank_gate, gate_enter) + nn(d_rank_upper, upper_enter)
     d_residual = grad_down.astype(f32) + norm_backward(
         residual, inverse_ffn, ffn_gain, d_normed_ffn
     )
     d_branch = d_residual.astype(bf16)
-    d_branch_all = gather_tokens(d_branch)
+    ranks_own = jnp.concatenate([rank_out, d_rank_gate, d_rank_upper, rank_down], axis=1)
+    d_branch_all, ranks_all = gather_tokens(6, d_branch, ranks_own)
+    hidden_late, ranks_all = lax.optimization_barrier((hidden, ranks_all))
+    down_part = nt(hidden_late, w2).astype(bf16)
+    d_branch_all, down_part = lax.optimization_barrier((d_branch_all, down_part))
+    down = lax.psum_scatter(down_part, "seq", scatter_dimension=0, tiled=True).astype(f32)
     d_rank_out = (nt(d_branch_all, out_leave) * select_all).astype(bf16)
     d_attn = (nt(d_branch_all, out_w) + nn(d_rank_out, out_enter)).astype(bf16)
     d_projected = attention_backward(slots, qs, kv, lse, d_attn, cosine, sine)
-    back_attn, back_rank_qkv = scatter_products([(d_projected, qkv_w, qkv_leave, True)], 5)
+    back_attn, back_rank_qkv = scatter_products([d_projected], [qkv_w], [True], [qkv_leave], [0], 5)
     d_rank_qkv = (back_rank_qkv * select_own).astype(bf16)
     d_normed_attn = back_attn + nn(d_rank_qkv, qkv_enter)
     input_grad = (d_residual + norm_backward(inputs_f, inverse_attn, attn_gain, d_normed_attn))[
         None
     ]
 
-    def reduced(partial, whole):
-        cols = []
-        if partial:
-            part = width // seq
-            stack = jnp.concatenate(
-                [p.astype(bf16).reshape(RANKS, seq, part) for p in partial], axis=2
-            ).transpose(1, 0, 2)
-            cols.append(lax.psum_scatter(stack, "seq", scatter_dimension=0, tiled=True)[0])
-        cols += [w.astype(bf16) for w in whole]
-        both = jnp.concatenate(cols, axis=1)
-        mine = lax.psum_scatter(both, "ad", scatter_dimension=0, tiled=True)
-        return lax.all_gather(mine, "seq", axis=0)
+    def reduced(sums):
+        both = jnp.concatenate([x.astype(bf16) for x in sums], axis=1)
+        return lax.psum_scatter(both, "ad", scatter_dimension=0, tiled=True)
 
     def unpack(arr, counts):
         out, at = [], 0
@@ -676,26 +751,32 @@
             at += c
         return out
 
-    wpart = width // seq
+    columns = lambda x: my_columns(x, wpart)
+    rank_out_all, d_rank_gate_all, d_rank_upper_all, rank_down_all = (
+        ranks_all[:, k * RANKS : (k + 1) * RANKS] for k in range(4)
+    )
+    normed_columns = columns(normed_ffn_all)
     early = reduced(
         [
-            tn(rank_out, d_branch),
-            tn(d_rank_gate, normed_ffn),
-            tn(d_rank_upper, normed_ffn),
-            tn(rank_down, grad_down),
-        ],
-        [
+            tn(rank_out_all, columns(d_branch_all)),
+            tn(d_rank_gate_all, normed_columns),
+            tn(d_rank_upper_all, normed_columns),
+            tn(rank_down_all, columns(grad_all)),
             tn(d_rank_out, attn),
             tn(rank_gate, d_gate),
             tn(rank_upper, d_upper),
             tn(d_rank_down, hidden),
-        ],
-    )
-    g_out_b, g_ia0, g_ia1, g_ob, g_out_a, g_ib0, g_ib1, g_oa = unpack(
-        early, [wpart] * 4 + [head_part] + [ff_part] * 3
-    )
-    late = reduced([tn(d_rank_qkv, normed_attn)], [tn(rank_qkv, d_projected)])
-    g_qkv_a, g_qkv_b = unpack(late, [wpart, qkv_part])
+        ]
+    )
+    (d_rank_qkv_all,) = gather_tokens(8, d_rank_qkv)
+    late_sums = [tn(d_rank_qkv_all, columns(normed_attn_all)), tn(rank_qkv, d_projected)]
+    late = reduced(late_sums)
+    (grads,) = gather_tokens(9, jnp.concatenate([early, late], axis=1))
+    grads = grads.reshape(seq, -1, grads.shape[1])
+    g_out_b, g_ia0, g_ia1, g_ob, g_out_a, g_ib0, g_ib1, g_oa, g_qkv_a, g_qkv_b = unpack(
+        grads, [wpart] * 4 + [head_part] + [ff_part] * 3 + [wpart, qkv_part]
+    )
+    output = (residual + down + nn(rank_down, down_leave)).astype(bf16)[None]
     return (
         output,
         input_grad,

time: 859 us -> 811 us (0.944)
  blocking collectives: 73.4 us -> 0 us
  waiting for transfers between devices: 121 us -> 60.7 us
  Pallas kernels: 429 us -> 487 us
  local copies, waits for them, and re-layouts: 39.5 us -> 61.2 us
  matrix products: 132 us -> 145 us
  starting transfers between devices: 9.59 us -> 0.32 us
    pallas_call x8 -> x12, Pallas kernels: 393 us -> 450 us  [the longest x7 229 us: gather_tokens(): pl.pallas_call(functools.partial(gather_kernel, count), out_shape=tuple((...]
    all_gather x6 -> x4, waiting for transfers between devices: 51.1 us -> 0.01 us  [all_rows(): lax.all_gather(part, 'ad', axis=1, tiled=True).reshape(-1, part.shape[2])]
    all_to_all x2 -> x0, blocking collectives: 36.9 us -> none  [column_shard(): part = lax.all_to_all(w, 'seq', split_axis=1, concat_axis=0, tiled=True)]
    all_gather x2 -> x0, blocking collectives: 36.5 us -> none  [the longest x1 26.4 us: stack_ad(): return lax.all_gather(a, 'ad', axis=0, tiled=True)]
    dot_general x6 -> x7, matrix products: 31.4 us -> 40.3 us  [nt(): lax.dot_general(a, b, (((1,), (1,)), ((), ())), preferred_element_type=f32)]
    all_to_all x2 -> x0, starting transfers between devices: 8.76 us -> none  [column_shard(): part = lax.all_to_all(w, 'seq', split_axis=1, concat_axis=0, tiled=True)]
    all_to_all x2 -> x0, waiting for transfers between devices: 8.66 us -> none  [column_shard(): part = lax.all_to_all(w, 'seq', split_axis=1, concat_axis=0, tiled=True)]
    unnamed x131 -> x129, local copies, waits for them, and re-layouts: 12.3 us -> 17.7 us
  transfers between devices with their start and end apart: 13 -> 8, of which waited for: 6 -> 3; matrix products, arithmetic and copies ran while one was open for 15% -> 20% of each run, Pallas kernels for 31% -> 34%
where the time goes in v3:
time: 811 us; the launch traced here: 802 us
  Pallas kernels  487 us (60%)
  matrix products  145 us (18%)
  local copies, waits for them, and re-layouts  61.2 us (8%)
  waiting for transfers between devices  60.7 us (7%)
  other arithmetic  32.3 us (4%)
  between operations  15.3 us (2%)
    pallas_call x7, Pallas kernels, gather_tokens(): pl.pallas_call(functools.partial(gather_kernel, count), out_shape=tuple((...  229 us
    pallas_call x3, Pallas kernels, scatter_products(): pl.pallas_call(functools.partial(scatter_kernel, tuple(modes), tuple(rank...  168 us
    dot_general x14, matrix products, nn(): return jnp.dot(a, b, preferred_element_type=f32)  89.3 us
    pallas_call x2, Pallas kernels, exchange_columns(): pl.pallas_call(functools.partial(exchange_kernel, count), out_shape=shape...  53.2 us
    dot_general x7, matrix products, nt(): lax.dot_general(a, b, (((1,), (1,)), ((), ())), preferred_element_type=f32)  40.3 us
    reduce_scatter x2, waiting for transfers between devices, reduced(): return lax.psum_scatter(both, 'ad', scatter_dimension=0, tiled=True)  37.8 us
    pallas_call x1, Pallas kernels, attention_backward(): pl.pallas_call(attention_backward_kernel, out_shape=jax.ShapeDtypeStruct(...  21.4 us
    reduce_scatter x1, waiting for transfers between devices, local(): lax.psum_scatter(down_part, 'seq', scatter_dimension=0, tiled=True)  21.1 us
  transfers between devices with their start and end apart: 8, of which 3 were waited for; matrix products, arithmetic and copies ran while one was open for 20% of the time, Pallas kernels for 34%

profile of v3, /device:TPU:0, one launch (start us, length us, event | category | flops | bytes accessed | tf_op | source)
XLA Modules:
  0.0 802.2 jit_solution(16900069790977733505)
XLA Ops:
  7.2 12.3 %shard_map.241 = bf16[8,64,512]{2,1,0:T(8,128)(2,1)} custom-call(bf16[64,4096]{1,0:T(8,128)(2,1)} %refs_0_.1), custom_call_target="tpu_custom_call" | custom-call | bytes 5242880 | tf_op jit(solution)/shard_map/pallas_call | solution.py:589
  37.6 40.9 %shard_map.244 = (bf16[8,64,1024]{2,1,0:T(8,128)(2,1)}, bf16[8,64,1024]{2,1,0:T(8,128)(2,1)}, bf16[8,64,1024]{2,1,0:T(8,128)(2,1)}) custom-call(bf16[64,8192]{1,0:T(8,128)(2,1)} %get-tuple-element.56.refs_0_, bf16[64,8192]{1,0:T(8,128)(2,1)} %get-tuple-element.57.refs_1_, bf16[64,8192]{1,0:T(8,128)(2,1)} %get-tuple-element.55.refs_2_), custom_call_target="tpu_custom_call" | custom-call | bytes 31457280 | tf_op jit(solution)/shard_map/pallas_call | solution.py:589
  82.2 44.4 %shard_map.240 = bf16[2048,2048]{1,0:T(8,128)(2,1)} custom-call(bf16[256,2048]{1,0:T(8,128)(2,1)} %fusion.14.refs_0_), custom_call_target="tpu_custom_call" | custom-call | bytes 41943040 | tf_op jit(solution)/shard_map/pallas_call | solution.py:382
  128.8 43.6 %shard_map.245 = bf16[2048,2048]{1,0:T(8,128)(2,1)} custom-call(bf16[256,2048]{1,0:T(8,128)(2,1)} %bitcast.135), custom_call_target="tpu_custom_call" | custom-call | bytes 41943040 | tf_op jit(solution)/shard_map/pallas_call | solution.py:382
  176.4 10.5 %fusion.58 = f32[2048,512]{1,0:T(8,128)} fusion(bf16[2048,2048]{1,0:T(8,128)(2,1)} %shard_map.240, bf16[2048,512]{1,0:T(8,128)(2,1)} %bitcast.162), kind=kOutput, calls=%fused_computation.151 | convolution fusion | flops 4294967296 | bytes 14680064 | tf_op jit(solution)/shard_map/dot_general | solution.py:34
  188.7 17.4 %shard_map.242 = bf16[1024,1280]{1,0:T(8,128)(2,1)} custom-call(bf16[128,1280]{1,0:T(8,128)(2,1)} %slice.150.refs_0_), custom_call_target="tpu_custom_call" | custom-call | bytes 13107200 | tf_op jit(solution)/shard_map/pallas_call | solution.py:382
  206.1 4.8 copy.57
  214.6 5.9 fusion.9
  224.1 5.0 convolution_add_fusion.2.proj_ref
  229.1 15.5 %attention_forward.1 = (bf16[2048,256]{1,0:T(8,128)(2,1)}, bf16[4096,128]{1,0:T(8,128)(2,1)}, bf16[2048,256]{1,0:T(8,128)(2,1)}, f32[4096,1]{1,0:T(8,128)}) custom-call(s32[16]{0:T(128)} %get-tuple-element.30.slot_ref, f32[2048,512]{1,0:T(8,128)} %convolution_add_fusion.2.proj_ref, f32[1152,128]{1,0:T(8,128)} %get-tuple-element.94.cos_ref, ...), custom_call_target="tpu_custom_call" | custom-call | flops 4000000000 | bytes 10485760 | tf_op jit(solution)/shard_map/attention_forward/pallas_call | solution.py:172
  245.3 48.3 %shard_map.243 = (f32[256,2048]{1,0:T(8,128)}, f32[256,128]{1,0:T(8,128)}) custom-call(bf16[2048,256]{1,0:T(8,128)(2,1)} %get-tuple-element.31.refs_0_, bf16[256,2048]{1,0:T(8,128)(2,1)} %reshape.182.refs_1_, bf16[128,256]{1,0:T(8,128)(2,1)} %slice.154.refs_2_), custom_call_target="tpu_custom_call" | custom-call | flops 42281701376 | bytes 2097152 | tf_op jit(solution)/shard_map/pallas_call | solution.py:504
  299.6 43.7 %shard_map.246 = bf16[2048,2048]{1,0:T(8,128)(2,1)} custom-call(bf16[256,2048]{1,0:T(8,128)(2,1)} %multiply_convert_fusion.3.refs_0_), custom_call_target="tpu_custom_call" | custom-call | bytes 41943040 | tf_op jit(solution)/shard_map/pallas_call | solution.py:382
  344.5 5.9 fusion.8
  352.1 4.7 fusion.51
  359.3 3.2 fusion.10
  362.5 14.8 %fusion.60 = f32[2048,1024]{1,0:T(8,128)} fusion(bf16[2048,2048]{1,0:T(8,128)(2,1)} %shard_map.246, bf16[2048,1024]{1,0:T(8,128)(2,1)} %bitcast.158), kind=kOutput, calls=%fused_computation.153 | convolution fusion | flops 8589934592 | bytes 20971520 | tf_op jit(solution)/shard_map/dot_general | solution.py:34
  377.3 14.5 %fusion.59 = f32[2048,1024]{1,0:T(8,128)} fusion(bf16[2048,2048]{1,0:T(8,128)(2,1)} %shard_map.246, bf16[2048,1024]{1,0:T(8,128)(2,1)} %bitcast.160), kind=kOutput, calls=%fused_computation.152 | convolution fusion | flops 8589934592 | bytes 20971520 | tf_op jit(solution)/shard_map/dot_general | solution.py:34
  391.8 15.8 %bitcast_add_fusion = f32[2048,1024]{1,0:T(8,128)} fusion(f32[2048,1024]{1,0:T(8,128)} %fusion.51, bf16[2048,2048]{1,0:T(8,128)(2,1)} %shard_map.245, bf16[2048,1024]{1,0:T(8,128)(2,1)} %bitcast.156), kind=kOutput, calls=%fused_computation | convolution fusion | flops 8592031744 | bytes 29360128 | tf_op jit(solution)/shard_map/dot_general | solution.py:34
  408.8 11.0 %multiply_convert_fusion = (bf16[2048,1024]{1,0:T(8,128)(2,1)}, bf16[2048,1024]{1,0:T(8,128)(2,1)}, bf16[2048,1024]{1,0:T(8,128)(2,1)}) fusion(f32[2048,1024]{1,0:T(8,128)S(1)} %convolution_add_fusion, f32[2048,1024]{1,0:T(8,128)} %bitcast_add_fusion, f32[2048,1024]{1,0:T(8,128)} %fusion.59, bf16[2048,128]{1,0:T(8,128)(2,1)S(1)} %copy-done.38, ...), kind=kOutput, calls=%fused_computation.1 | convolution fusion | flops 570425344 | bytes 38535168 | tf_op jit(solution)/shard_map/dot_general | solution.py:34
  419.9 69.2 %shard_map.247 = (f32[256,2048]{1,0:T(8,128)}, f32[256,384]{1,0:T(8,128)}) custom-call(bf16[2048,1024]{1,0:T(8,128)(2,1)} %get-tuple-element.53.refs_0_, bf16[2048,1024]{1,0:T(8,128)(2,1)} %get-tuple-element.54.refs_1_, bf16[2048,1024]{1,0:T(8,128)(2,1)} %get-tuple-element.41.refs_2_, bf16[2048,1024]{1,0:T(8,128)(2,1)} %bitcast.159, ...), custom_call_target="tpu_custom_call" | custom-call | flops 70601637888 | bytes 25165824 | tf_op jit(solution)/shard_map/pallas_call | solution.py:504
  497.6 53.0 %shard_map.248 = (bf16[2048,2048]{1,0:T(8,128)(2,1)}, bf16[2048,512]{1,0:T(8,128)(2,1)}) custom-call(bf16[256,2048]{1,0:T(8,128)(2,1)} %get-tuple-element.50.refs_0_, bf16[256,512]{1,0:T(8,128)(2,1)} %pad_maximum_fusion.3.refs_1_), custom_call_target="tpu_custom_call" | custom-call | bytes 52428800 | tf_op jit(solution)/shard_map/pallas_call | solution.py:382
  550.6 14.5 %convolution_convert_fusion = bf16[2048,2048]{1,0:T(8,128)(2,1)} fusion(bf16[2048,1024]{1,0:T(8,128)(2,1)} %get-tuple-element.41.refs_2_, bf16[2048,1024]{1,0:T(8,128)(2,1)} %bitcast.157), kind=kOutput, calls=%fused_computation.6 | convolution fusion | flops 8594128896 | bytes 16777216 | tf_op jit(solution)/shard_map/dot_general | solution.py:38
  565.2 5.9 fusion.7
  582.8 21.4 %attention_backward.1.refs_0_ = bf16[2048,512]{1,0:T(8,128)(2,1)} custom-call(s32[16]{0:T(128)} %get-tuple-element.30.slot_ref, bf16[4096,128]{1,0:T(8,128)(2,1)} %get-tuple-element.43.qs_ref, bf16[2048,256]{1,0:T(8,128)(2,1)} %get-tuple-element.44.kv_ref, f32[4096,1]{1,0:T(8,128)} %get-tuple-element.45.lse_ref, bf16[2048,256]{1,0:T(8,128)(2,1)} %fusion.4.grad_ref, ...), custom_call_target="tpu_custom_call" | custom-call | flops 8999999488 | bytes 10485760 | tf_op jit(solution)/shard_map/attention_backward/pallas_call | solution.py:253
  606.2 50.4 %shard_map.249 = (f32[256,2048]{1,0:T(8,128)}, f32[256,128]{1,0:T(8,128)}) custom-call(bf16[2048,512]{1,0:T(8,128)(2,1)} %attention_backward.1.refs_0_, bf16[2048,512]{1,0:T(8,128)(2,1)} %bitcast.163, bf16[128,512]{1,0:T(8,128)(2,1)} %slice.152.refs_2_), custom_call_target="tpu_custom_call" | custom-call | flops 44563402752 | bytes 4194304 | tf_op jit(solution)/shard_map/pallas_call | solution.py:504
  658.3 9.5 %shard_map.250 = bf16[2048,128]{1,0:T(8,128)(2,1)} custom-call(bf16[256,128]{1,0:T(8,128)(2,1)} %multiply_convert_fusion.4.refs_0_), custom_call_target="tpu_custom_call" | custom-call | bytes 2621440 | tf_op jit(solution)/shard_map/pallas_call | solution.py:382
  670.3 3.8 fusion.21
  681.3 8.9 %reduce-scatter.8.cloned.1.call-done = bf16[32,768]{1,0:T(8,128)(2,1)} async-done(((bf16[128,768]{1,0:T(8,128)(2,1)}), bf16[32,768]{1,0:T(8,128)(2,1)}) %reduce-scatter.8.cloned.1.call-update) | async-done | bytes 49168 | tf_op jit(solution)/shard_map/reduce_scatter | solution.py:744
  690.1 28.9 %reduce-scatter.6.cloned.1.call-done = bf16[32,4352]{1,0:T(8,128)(2,1)} async-done(((bf16[128,4352]{1,0:T(8,128)(2,1)}), bf16[32,4352]{1,0:T(8,128)(2,1)}) %reduce-scatter.6.cloned.1.call-update) | async-done | bytes 278544 | tf_op jit(solution)/shard_map/reduce_scatter | solution.py:744
  720.7 17.6 %shard_map.251 = bf16[256,5120]{1,0:T(8,128)(2,1)} custom-call(bf16[32,5120]{1,0:T(8,128)(2,1)} %pad_maximum_fusion.2.refs_0_), custom_call_target="tpu_custom_call" | custom-call | bytes 13107200 | tf_op jit(solution)/shard_map/pallas_call | solution.py:382
  768.8 2.7 maximum_convert_fusion
  771.4 21.1 %reduce-scatter.4.cloned.1.call-done = bf16[256,2048]{1,0:T(8,128)(2,1)} async-done(((bf16[2048,2048]{1,0:T(8,128)(2,1)}), bf16[256,2048]{1,0:T(8,128)(2,1)}) %reduce-scatter.4.cloned.1.call-update) | async-done | bytes 1048592 | tf_op jit(solution)/shard_map/reduce_scatter | solution.py:731
  (237 shorter events, 117.9 us)
Async XLA Ops:
  7.2 169.2 %all-gather.6.cloned.1.call-start = ((), (), s32[]{:S(2)}) async-start(), calls=%async_computation.3 | async-start | bytes 2621440 | tf_op jit(solution)/shard_map/all_gather | solution.py:606
  19.5 167.4 %all-gather.8.cloned.1.call-start = ((), (), s32[]{:S(2)}) async-start(), calls=%async_computation.4 | async-start | bytes 2949120 | tf_op jit(solution)/shard_map/all_gather | solution.py:642
  19.6 16.3 %copy-start.13 = (bf16[64,3,8192]{2,0,1:T(8,128)(2,1)S(1)}, bf16[64,3,8192]{2,0,1:T(8,128)(2,1)}, u32[]{:S(2)}) copy-start(bf16[64,3,8192]{2,0,1:T(8,128)(2,1)} %param.25) | copy-start | bytes 9437188
  35.8 326.7 %all-gather.14.cloned.1.call-start = ((), (), s32[]{:S(2)}) async-start(), calls=%async_computation.7 | async-start | bytes 5242880 | tf_op jit(solution)/shard_map/all_gather | solution.py:606
  78.6 298.7 %all-gather.12.cloned.1.call-start = ((), (), s32[]{:S(2)}) async-start(), calls=%async_computation.6 | async-start | bytes 5242880 | tf_op jit(solution)/shard_map/all_gather | solution.py:606
  79.2 312.6 %all-gather.10.cloned.1.call-start = ((), (), s32[]{:S(2)}) async-start(), calls=%async_computation.5 | async-start | bytes 5242880 | tf_op jit(solution)/shard_map/all_gather | solution.py:606
  79.8 610.4 %reduce-scatter.8.cloned.1.call-start = ((), (), s32[]{:S(2)}) async-start(), calls=%async_computation.10 | async-start | bytes 245760 | tf_op jit(solution)/shard_map/reduce_scatter | solution.py:744
  79.8 279.4 %copy-start.53 = (s32[128]{0:T(128)}, s32[128]{0:T(128)S(1)}, u32[]{:S(2)}) copy-start(s32[128]{0:T(128)S(1)} %and_select_fusion) | copy-start | bytes 1540
  80.0 279.2 %copy-start.45 = (s32[2048]{0:T(1024)}, s32[2048]{0:T(1024)S(1)}, u32[]{:S(2)}) copy-start(s32[2048]{0:T(1024)S(1)} %broadcast_bitcast_fusion) | copy-start | bytes 24580
  214.6 5.9 copy-start.18
  229.1 15.5 %copy-start.9 = (bf16[128,9216]{1,0:T(8,128)(2,1)S(1)}, bf16[128,9216]{1,0:T(8,128)(2,1)}, u32[]{:S(2)}) copy-start(bf16[128,9216]{1,0:T(8,128)(2,1)} %all-gather.8.cloned.1.call-done) | copy-start | bytes 7077892
  299.6 43.7 %copy-start.26 = (bf16[1,128,8,256]{1,2,3,0:T(8,128)(2,1)S(1)}, bf16[1,128,8,256]{1,2,3,0:T(8,128)(2,1)}, u32[]{:S(2)}) copy-start(bf16[1,128,8,256]{1,2,3,0:T(8,128)(2,1)} %get-tuple-element.68) | copy-start | bytes 1572868
  299.6 43.8 %copy-start.25 = (bf16[1,128,8,256]{1,2,3,0:T(8,128)(2,1)S(1)}, bf16[1,128,8,256]{1,2,3,0:T(8,128)(2,1)}, u32[]{:S(2)}) copy-start(bf16[1,128,8,256]{1,2,3,0:T(8,128)(2,1)} %get-tuple-element.67) | copy-start | bytes 1572868
  343.4 13.4 %copy-start.22 = (bf16[1,128,8,256]{1,3,2,0:T(8,128)(2,1)}, bf16[1,128,8,256]{1,3,2,0:T(8,128)(2,1)S(1)}, u32[]{:S(2)}) copy-start(bf16[1,128,8,256]{1,3,2,0:T(8,128)(2,1)S(1)} %copy.64) | copy-start | bytes 1572868
  343.5 15.8 %copy-start.20 = (bf16[1,128,8,256]{1,3,2,0:T(8,128)(2,1)}, bf16[1,128,8,256]{1,3,2,0:T(8,128)(2,1)S(1)}, u32[]{:S(2)}) copy-start(bf16[1,128,8,256]{1,3,2,0:T(8,128)(2,1)S(1)} %copy.63) | copy-start | bytes 1572868
  344.5 5.9 copy-start.16
  350.4 6.4 copy-start.11
  351.2 5.6 slice-start
  359.2 48.3 %copy-start.14 = (bf16[2048,128]{1,0:T(8,128)(2,1)}, bf16[2048,128]{1,0:T(8,128)(2,1)S(1)}, u32[]{:S(2)}) copy-start(bf16[2048,128]{1,0:T(8,128)(2,1)S(1)} %fusion.11) | copy-start | bytes 1572868
  391.8 15.8 %copy-start.5 = (f32[2048,1024]{1,0:T(8,128)S(1)}, f32[2048,1024]{1,0:T(8,128)}, u32[]{:S(2)}) copy-start(f32[2048,1024]{1,0:T(8,128)} %fusion.60) | copy-start | bytes 25165828
  419.9 71.3 %copy-start.23 = (bf16[1,128,8,256]{1,3,2,0:T(8,128)(2,1)S(1)}, bf16[1,128,8,256]{1,3,2,0:T(8,128)(2,1)}, u32[]{:S(2)}) copy-start(bf16[1,128,8,256]{1,3,2,0:T(8,128)(2,1)} %copy-done.22) | copy-start | bytes 1572868
  550.6 14.5 %copy-start.19 = (bf16[1,128,8,256]{1,3,2,0:T(8,128)(2,1)S(1)}, bf16[1,128,8,256]{1,3,2,0:T(8,128)(2,1)}, u32[]{:S(2)}) copy-start(bf16[1,128,8,256]{1,3,2,0:T(8,128)(2,1)} %copy.59) | copy-start | bytes 1572868
  550.6 14.5 %copy-start.46 = (s32[2048]{0:T(1024)S(1)}, s32[2048]{0:T(1024)}, u32[]{:S(2)}) copy-start(s32[2048]{0:T(1024)} %copy-done.45) | copy-start | bytes 24580
  550.6 14.5 %copy-start.54 = (s32[128]{0:T(128)S(1)}, s32[128]{0:T(128)}, u32[]{:S(2)}) copy-start(s32[128]{0:T(128)} %copy-done.53) | copy-start | bytes 1540
  565.1 5.9 copy-start.32
  565.1 6.1 copy-start.40
  582.8 21.4 %copy-start.29 = (bf16[2048,128]{1,0:T(8,128)(2,1)S(1)}, bf16[2048,128]{1,0:T(8,128)(2,1)}, u32[]{:S(2)}) copy-start(bf16[2048,128]{1,0:T(8,128)(2,1)} %copy-done.28) | copy-start | bytes 1572868
  656.6 13.7 %copy-start.39 = (bf16[2048,128]{1,0:T(8,128)(2,1)S(1)}, bf16[2048,128]{1,0:T(8,128)(2,1)}, u32[]{:S(2)}) copy-start(bf16[2048,128]{1,0:T(8,128)(2,1)} %fusion.10) | copy-start | bytes 1572868
  670.2 48.8 %reduce-scatter.6.cloned.1.call-start = ((), (), s32[]{:S(2)}) async-start(), calls=%async_computation.9 | async-start | bytes 1392640 | tf_op jit(solution)/shard_map/reduce_scatter | solution.py:744
  675.6 116.9 %reduce-scatter.4.cloned.1.call-start = ((), (), s32[]{:S(2)}) async-start(), calls=%async_computation.8 | async-start | bytes 9437184 | tf_op jit(solution)/shard_map/reduce_scatter | solution.py:731
  757.6 5.3 copy-start.33
  766.1 26.5 %copy-start.17 = (bf16[1,128,8,256]{1,3,2,0:T(8,128)(2,1)S(1)}, bf16[1,128,8,256]{1,3,2,0:T(8,128)(2,1)}, u32[]{:S(2)}) copy-start(bf16[1,128,8,256]{1,3,2,0:T(8,128)(2,1)} %copy-done.16) | copy-start | bytes 1572868
  (36 other events, 84.4 us)
Sparse Core Ops, SparseCore 0:
  19.7 47.0 all-gather.5
  68.9 48.7 all-gather.7
  119.3 79.4 all-gather.13
  200.3 79.2 all-gather.11
  280.9 79.2 all-gather.9
  670.3 19.7 reduce-scatter.7
  692.4 26.5 reduce-scatter.5
  722.5 69.9 reduce-scatter.3
